TPU v7x, 128 devices: a whole 4x4x4 slice. The times are simulated.
128 devices in a mesh: seq: 32 (over y, x, core), tp: 4 (over z).
Axes of the slice: x: 4, y: 4, z: 4, core: 2. Of those that a mesh axis runs over, the one named last changes fastest.
Arguments:
- hidden: bfloat16 [32768, 2560], P('seq', 'tp'), may hold values from -6 to 6
- gate_proj: bfloat16 [2560, 5120], P(None, 'tp'), may hold values from -0.125 to 0.125
- input_proj: bfloat16 [2560, 5120], P(None, 'tp'), may hold values from -0.125 to 0.125
- bc_proj: bfloat16 [2560, 256], replicated, may hold values from -0.125 to 0.125
- step_proj: bfloat16 [2560, 80], P(None, 'tp'), may hold values from -0.125 to 0.125
- step_bias: float32 [80], P('tp'), may hold values from -16 to -3
- decay_log: float32 [80], P('tp'), may hold values from 0 to 2.78
- conv_weight: float32 [4, 5120], P(None, 'tp'), may hold values from -3 to 3
- conv_bias: float32 [5120], P('tp'), may hold values from -3 to 3
- bc_conv_weight: float32 [4, 256], replicated, may hold values from -3 to 3
- bc_conv_bias: float32 [256], replicated, may hold values from -3 to 3
- skip_gain: float32 [80], P('tp'), may hold values from 0.5 to 2
- norm_gain: float32 [5120], P('tp'), may hold values from 0.1 to 1.9
- out_proj: bfloat16 [5120, 2560], P('tp'), may hold values from -0.078125 to 0.078125
- amax_history: float32 [16], replicated, may hold values from 1.5 to 4
Outputs:
- mixed: bfloat16 [32768, 2560], P('seq', 'tp')
- new_history: float32 [16], replicated
All inputs are finite; a program needn't handle non-finite values.
Results may differ from a plain program's by a relative error of at most 0.015.
Values may be sent and summed in bfloat16 or wider, within the bound.
A program may use at most 192 MiB of HBM per device.

v0:
```python
import jax
import jax.numpy as jnp
from jax import lax
from jax.sharding import Mesh
from jax.sharding import PartitionSpec as P

BLOCK = 256
INNER = 5120
SEQ = ("seq_0", "seq_1", "seq_2")


QMAX = 448.0
EPS = 1e-05


def shifted(x, axis, by):
    size = lax.axis_size(axis)
    pairs = [(i, i + by) for i in range(size) if 0 <= i + by < size]
    return lax.ppermute(x, axis, pairs)


def nothing_yet(x, identity):
    return jax.tree.map(
        lambda part, zero: jnp.zeros_like(part) + jnp.asarray(zero, part.dtype), x, identity
    )


def entering(x, axes, combine, identity):
    before = start = nothing_yet(x, identity)
    subtotal = x
    for axis in reversed(axes):
        size, here = (lax.axis_size(axis), lax.axis_index(axis))
        pieces = jax.tree.map(
            lambda part, kind: lax.all_gather(part.astype(kind), axis),
            subtotal,
            (jnp.bfloat16, jnp.bfloat16),
        )
        inside, subtotal = (start, start)
        for k in range(size):
            passed = k < here
            subtotal = combine(
                subtotal, jax.tree.map(lambda part, own: part[k].astype(own.dtype), pieces, x)
            )
            inside = jax.tree.map(lambda new, old: jnp.where(passed, new, old), subtotal, inside)
        before = combine(inside, before)
    return before


def from_everyone(x, axis):
    size = lax.axis_size(axis)
    return lax.all_to_all(jnp.broadcast_to(x[None], (size, *x.shape)), axis, 0, 0, tiled=True)


def gathered_once(x, axis):
    leaves = jax.tree.leaves(x)
    turns = sorted(range(len(leaves)), key=lambda k: -leaves[k].size)
    width = (1, *leaves[turns[0]].shape)[-1]
    lines = [
        jnp.pad(leaves[k].reshape(-1), (0, -leaves[k].size % width)).reshape(-1, width)
        for k in turns
    ]
    both, at, found = (from_everyone(jnp.concatenate(lines), axis), 0, {})
    for k, line in zip(turns, lines):
        section = both[:, at : at + len(line)].reshape(len(both), -1)
        found[k] = section[:, : leaves[k].size].reshape(-1, *leaves[k].shape)
        at += len(line)
    numbers = iter(range(len(leaves)))
    return jax.tree.map(lambda _: found[next(numbers)], x)


def collected_alike(x, axis):
    leaves, found = (jax.tree.leaves(x), {})
    for first, a in enumerate(leaves):
        if first not in found:
            alike = [k for k, b in enumerate(leaves) if b.dtype == a.dtype]
            got = (
                gathered_once([leaves[k] for k in alike], axis)
                if len(alike) > 1
                else [from_everyone(a, axis)]
            )
            for k, b in zip(alike, got):
                found[k] = b
    numbers = iter(range(len(leaves)))
    return jax.tree.map(lambda _: found[next(numbers)], x)


def combined_pairwise(pieces, combine):
    while len(jax.tree.leaves(pieces)[0]) > 1:
        pieces = jax.vmap(combine)(
            *(jax.tree.map(lambda part: part[side::2], pieces) for side in (0, 1))
        )
    return jax.tree.map(lambda part: part[0], pieces)


def combined_all(x, axis, combine):
    pieces = collected_alike(x, axis)
    return combined_pairwise(pieces, combine)


def of_everyone(x, axis):
    everything = from_everyone(x, axis)
    return jnp.max(everything, axis=0)


def conv_silu(pre_conv, rim_rows, weight, conv_shift):
    row_count = pre_conv.shape[0]
    kernel = weight.shape[0]
    padded = jnp.concatenate([rim_rows, pre_conv], axis=0)
    running = jnp.zeros(pre_conv.shape, jnp.float32)
    for offset in range(kernel):
        running = running + weight[offset] * padded[offset : offset + row_count].astype(jnp.float32)
    return jax.nn.silu(running + conv_shift).astype(jnp.bfloat16)


def ssd_block(carry_state, block_data):
    x_block, b_block, c_block, step_block, decay_block = block_data
    length = x_block.shape[0]
    head_count = carry_state.shape[0]
    head_width = carry_state.shape[1]
    cum_decay = jnp.cumsum(decay_block, axis=1)
    scores = jnp.dot(c_block, b_block.T, preferred_element_type=jnp.float32)
    causal = lax.broadcasted_iota(jnp.int32, (length, length), 0) >= lax.broadcasted_iota(
        jnp.int32, (length, length), 1
    )
    decay_gap = cum_decay[:, :, None] - cum_decay[:, None, :]
    decay_mask = jnp.where(causal, jnp.exp(jnp.where(causal, decay_gap, 0.0)), 0.0)
    weights = (scores[None] * decay_mask * step_block[:, None, :]).astype(jnp.bfloat16)
    x_heads = x_block.reshape(length, head_count, head_width)
    intra_out = jnp.einsum("hts,shp->htp", weights, x_heads, preferred_element_type=jnp.float32)
    inter_out = jnp.exp(cum_decay)[:, :, None] * jnp.einsum(
        "tn,hpn->htp", c_block.astype(jnp.float32), carry_state
    )
    tail_decay = jnp.exp(cum_decay[:, -1:] - cum_decay) * step_block
    x_weighted = (tail_decay.T[:, :, None] * x_heads.astype(jnp.float32)).astype(jnp.bfloat16)
    update = jnp.einsum("shp,sn->hpn", x_weighted, b_block, preferred_element_type=jnp.float32)
    next_state = jnp.exp(cum_decay[:, -1])[:, None, None] * carry_state + update
    block_out = (intra_out + inter_out).transpose(1, 0, 2).reshape(length, head_count * head_width)
    return (next_state, block_out)


def chain(earlier, later):
    return (earlier[0] + later[0], jnp.exp(later[0])[..., None, None] * earlier[1] + later[1])


def joint(first, second):
    return (first[0] + second[0], jnp.maximum(first[1], second[1]))


def shards(
    hidden,
    gate_proj,
    input_proj,
    bc_proj,
    step_proj,
    step_bias,
    decay_log,
    conv_weight,
    conv_bias,
    bc_conv_weight,
    bc_conv_bias,
    skip_gain,
    norm_gain,
    out_proj,
    amax_history,
):
    row_count = hidden.shape[0]
    inner_local = gate_proj.shape[1]
    state_width = bc_proj.shape[1] // 2
    head_count = step_proj.shape[1]
    head_width = inner_local // head_count
    kernel = conv_weight.shape[0]
    matrices = (gate_proj, input_proj, bc_proj, step_proj)
    piece = lax.all_gather(hidden, "tp", axis=1, tiled=True)
    gate_raw, x_raw, bc_raw, step_raw = tuple(
        (jnp.dot(piece, matrix, preferred_element_type=jnp.float32) for matrix in matrices)
    )
    gate_in = gate_raw.astype(jnp.bfloat16)
    x_pre = x_raw.astype(jnp.bfloat16)
    bc_pre = bc_raw.astype(jnp.bfloat16)
    x_rim, bc_rim = shifted(
        (x_pre[row_count - kernel + 1 :], bc_pre[row_count - kernel + 1 :]), SEQ, 1
    )
    x_conv = conv_silu(x_pre, x_rim, conv_weight, conv_bias)
    bc_conv = conv_silu(bc_pre, bc_rim, bc_conv_weight, bc_conv_bias)
    b_in = bc_conv[:, :state_width]
    c_out = bc_conv[:, state_width:]
    step_size = jax.nn.softplus(step_raw + step_bias)
    log_decay = step_size * -jnp.exp(decay_log)
    blocks = row_count // BLOCK
    stacked = (
        x_conv.reshape(blocks, BLOCK, inner_local),
        b_in.reshape(blocks, BLOCK, state_width),
        c_out.reshape(blocks, BLOCK, state_width),
        step_size.reshape(blocks, BLOCK, head_count).transpose(0, 2, 1),
        log_decay.reshape(blocks, BLOCK, head_count).transpose(0, 2, 1),
    )
    zero_state = jnp.zeros((head_count, head_width, state_width), jnp.float32)
    local_state, block_outs = lax.scan(ssd_block, zero_state, stacked)
    total_decay = jnp.sum(log_decay, axis=0)
    entry_decay, incoming = entering(
        (total_decay, local_state), SEQ, chain, (jnp.zeros_like(total_decay), zero_state)
    )
    reach = jnp.exp(jnp.cumsum(log_decay, axis=0))
    carried = jnp.einsum("tn,hpn->thp", c_out.astype(jnp.float32), incoming)
    ssm_out = block_outs.reshape(row_count, inner_local) + (reach[:, :, None] * carried).reshape(
        row_count, inner_local
    )
    x_heads = x_conv.reshape(row_count, head_count, head_width).astype(jnp.float32)
    ssm_out = ssm_out + (skip_gain[:, None] * x_heads).reshape(row_count, inner_local)
    gated = ssm_out * jax.nn.silu(gate_in.astype(jnp.float32))
    local_squares = jnp.sum(gated * gated, axis=1)
    row_peak = jnp.max(jnp.abs(gated * norm_gain), axis=1)
    squares, row_top = combined_all((local_squares, row_peak), "tp", joint)
    inv_rms = lax.rsqrt(squares / INNER + EPS)
    normed = gated * inv_rms[:, None] * norm_gain
    peak_value = of_everyone(jnp.max(row_top * inv_rms), SEQ)
    scale = QMAX / jnp.max(amax_history)
    quant = jnp.clip(normed * scale, -QMAX, QMAX).astype(jnp.bfloat16)
    partial_value = jnp.dot(quant, out_proj, preferred_element_type=jnp.float32)
    summed = lax.psum_scatter(
        partial_value.astype(jnp.bfloat16), "tp", scatter_dimension=1, tiled=True
    ).astype(jnp.float32)
    mixed = (summed / scale).astype(jnp.bfloat16)
    new_history = jnp.concatenate([jnp.reshape(peak_value, (1,)), amax_history[:-1]])
    return (mixed, new_history)


def solution(mesh):
    finer = Mesh(mesh.devices.reshape(4, 4, 2, mesh.shape["tp"]), ("seq_0", "seq_1", "seq_2", "tp"))
    in_specs = (
        P(SEQ, "tp"),
        P(None, "tp"),
        P(None, "tp"),
        P(),
        P(None, "tp"),
        P("tp"),
        P("tp"),
        P(None, "tp"),
        P("tp"),
        P(),
        P(),
        P("tp"),
        P("tp"),
        P("tp", None),
        P(),
    )
    out_specs = (P(SEQ, "tp"), P())
    return jax.shard_map(
        shards, mesh=finer, in_specs=in_specs, out_specs=out_specs, check_vma=False
    )
```

profile of v0, /device:TPU:0, one launch (start us, length us, event | category | flops | bytes accessed | tf_op | source)
XLA Modules:
  0.0 331.6 jit_solution(15634064660990956811)
XLA Ops:
  8.0 1.2 dynamic-slice
  9.9 0.9 slice_reduce_fusion.5
  11.5 0.8 fusion.140
  12.3 57.0 %all-gather.8.cloned.1.call-done = bf16[1024,2560]{1,0:T(8,128)(2,1)} async-done(((bf16[1024,640]{1,0:T(8,128)(2,1)}), bf16[1024,2560]{1,0:T(8,128)(2,1)}) %all-gather.8.cloned.1.call-update) | async-done | bytes 5242896 | tf_op jit(solution)/shard_map/all_gather | solution.py:173
  69.3 4.1 %convolution_convert_fusion.3 = bf16[1024,256]{1,0:T(8,128)(2,1)S(1)} fusion(bf16[1024,2560]{1,0:T(8,128)(2,1)} %all-gather.8.cloned.1.call-done, bf16[2560,256]{1,0:T(8,128)(2,1)S(1)} %copy-done), kind=kOutput, calls=%fused_computation.68 | convolution fusion | flops 1342439424 | bytes 7077888 | tf_op jit(solution)/shard_map/dot_general | solution.py:175
  73.5 1.7 collective-permute-start.1
  75.3 10.0 %convolution_convert_fusion.2 = bf16[1024,1280]{1,0:T(8,128)(2,1)S(1)} fusion(bf16[1024,2560]{1,0:T(8,128)(2,1)S(1)} %copy-done.3, bf16[2560,1280]{1,0:T(8,128)(2,1)} %param.19), kind=kOutput, calls=%fused_computation.55 | convolution fusion | flops 6712197120 | bytes 14417920 | tf_op jit(solution)/shard_map/dot_general | solution.py:175
  85.3 4.0 %collective-permute-start = (bf16[3,1280]{1,0:T(4,128)(2,1)S(1)}, bf16[3,1280]{1,0:T(4,128)(2,1)S(1)}, u32[]{:S(2)}, u32[]{:S(2)}) collective-permute-start(bf16[3,1280]{1,0:T(4,128)(2,1)S(1)} %slice.235), channel_id=1, source_target_pairs={{0,4},{4,8},{8,12},{12,16},{16,20},{20,24},{24,28},{28,32},{32,36}... | collective-permute-start | bytes 23048 | tf_op jit(solution)/shard_map/ppermute | solution.py:19
  89.3 2.2 fusion.111
  92.0 2.4 all-reduce
  96.6 8.2 %multiply_convert_fusion.4 = bf16[1024,1280]{1,0:T(8,128)(2,1)} fusion(bf16[1024,1280]{1,0:T(8,128)(2,1)} %copy-done.6, bf16[3,1280]{1,0:T(4,128)(2,1)S(1)} %collective-permute-done, f32[1280]{0:T(1024)S(1)} %copy-done.11, f32[1280]{0:T(1024)S(1)} %get-tuple-element.126, f32[1280]{0:T(1024)S(1)} %get-tuple-element.127, f32[1280]{0:T(1024)S(1)} %get-tuple-element.125, ...), kind=kLoop, calls=%fused_computation.53 | loop fusion | flops 34078720 | bytes 5276160 | tf_op jit(solution)/shard_map/convert_element_type | solution.py:112
  104.8 47.1 %while.13 = (s32[]{:T(128)}, f32[20,64,128]{2,1,0:T(8,128)S(1)}, f32[4,256,1280]{2,1,0:T(8,128)}, f32[4,20,256]{2,1,0:T(8,128)}, f32[4,20,256]{2,1,0:T(8,128)}, ...) while((s32[]{:T(128)}, f32[20,64,128]{2,1,0:T(8,128)S(1)}, ...), condition=%wide.region_3.4_spmd.clone, body=%wide.region_0.3_spmd.clone.sunk | while | flops 363210816 | bytes 22548344 | solution.py:198
  104.8 0.8 constant_dynamic-slice_fusion.5
  106.7 1.4 multiply_bitcast_fusion.3
  108.4 1.1 constant_dynamic-slice_fusion.4
  109.8 1.7 fusion.172
  111.5 1.1 fusion.173
  113.0 1.2 constant_dynamic-update-slice_fusion.2
  114.2 1.2 fusion.170
  115.4 1.2 convolution_add_fusion.3
  116.6 0.8 constant_dynamic-slice_fusion.5
  118.5 1.4 multiply_bitcast_fusion.3
  120.1 1.1 constant_dynamic-slice_fusion.4
  121.6 1.7 fusion.172
  123.3 1.1 fusion.173
  124.8 1.1 constant_dynamic-update-slice_fusion.2
  125.9 1.2 fusion.170
  127.1 1.2 convolution_add_fusion.3
  128.4 0.8 constant_dynamic-slice_fusion.5
  130.3 1.4 multiply_bitcast_fusion.3
  131.9 1.1 constant_dynamic-slice_fusion.4
  133.3 1.7 fusion.172
  135.0 1.1 fusion.173
  136.5 1.3 constant_dynamic-update-slice_fusion.2
  137.8 1.2 fusion.170
  139.0 1.2 convolution_add_fusion.3
  140.3 0.8 constant_dynamic-slice_fusion.5
  142.2 1.4 multiply_bitcast_fusion.3
  143.8 1.1 constant_dynamic-slice_fusion.4
  145.2 1.7 fusion.172
  146.9 1.1 fusion.173
  148.4 1.2 constant_dynamic-update-slice_fusion.2
  149.5 1.2 fusion.170
  150.8 1.2 convolution_add_fusion.3
  152.1 2.6 all-gather.1
  154.7 1.0 fusion.66
  155.8 9.7 %all-gather.2 = bf16[4,1,20]{2,1,0:T(2,128)(2,1)S(1)} all-gather(bf16[1,1,20]{2,1,0:T(2,128)(2,1)} %get-tuple-element.170), channel_id=1, replica_groups=mesh['seq_0'=4,'seq_1'=4,'seq_2'=2,'tp'=4] {'seq_1'}, dimensions={0}, use_global_device_ids=true | all-gather | bytes 200 | tf_op jit(solution)/shard_map/all_gather | solution.py:34
  165.6 15.1 %all-gather.10.cloned.1.call-done = bf16[4,20,64,128]{3,2,1,0:T(8,128)(2,1)} async-done(((bf16[1,20,64,128]{3,2,1,0:T(8,128)(2,1)}), bf16[4,20,64,128]{3,2,1,0:T(8,128)(2,1)}) %all-gather.10.cloned.1.call-update) | async-done | bytes 1310736 | tf_op jit(solution)/shard_map/all_gather | solution.py:34
  180.6 2.4 fusion.60
  183.3 5.6 %reduce-window.16 = f32[20,8,128]{2,1,0:T(8,128)S(1)} reduce-window(f32[20,8,128]{2,1,0:T(8,128)S(1)} %slice.273, f32[]{:T(128)} %constant.37.clone.1), window={size=1x1x128 pad=0_0x0_0x127_0}, to_apply=%region_4.5 | reduce-window | flops 2600960 | bytes 163844 | tf_op jit(solution)/shard_map/reduce-window.2
  189.4 9.8 %all-gather.3 = bf16[4,1,20]{2,1,0:T(2,128)(2,1)S(1)} all-gather(bf16[1,1,20]{2,1,0:T(2,128)(2,1)S(1)} %get-tuple-element.164), channel_id=1, replica_groups=mesh['seq_0'=4,'seq_1'=4,'seq_2'=2,'tp'=4] {'seq_0'}, dimensions={0}, use_global_device_ids=true | all-gather | bytes 200 | tf_op jit(solution)/shard_map/all_gather | solution.py:34
  199.3 9.4 %all-gather.12.cloned.1.call-done = bf16[4,20,64,128]{3,2,1,0:T(8,128)(2,1)} async-done(((bf16[1,20,64,128]{3,2,1,0:T(8,128)(2,1)}), bf16[4,20,64,128]{3,2,1,0:T(8,128)(2,1)}) %all-gather.12.cloned.1.call-update) | async-done | bytes 1310736 | tf_op jit(solution)/shard_map/all_gather | solution.py:34
  208.6 5.8 %broadcast_multiply_fusion = f32[1024,20,64]{0,2,1:T(8,128)} fusion(f32[1024,20]{0,1:T(8,128)S(1)} %bitcast.302, bf16[4,20,64,128]{3,2,1,0:T(8,128)(2,1)} %all-gather.12.cloned.1.call-done, f32[20]{0:T(128)S(1)} %get-tuple-element.171, f32[20]{0:T(128)S(1)} %get-tuple-element.169, f32[20]{0:T(128)S(1)} %get-tuple-element.168, ...), kind=kOutput, calls=%fused_computation.66 | convolution fusion | flops 343572480 | bytes 8886282 | tf_op jit(solution)/shard_map/tn,hpn->thp/dot_general | solution.py:204
  214.5 5.9 %copy.71 = f32[1024,1280]{1,0:T(8,128)} copy(f32[1024,1280]{0,1:T(8,128)} %bitcast.291) | data formatting | bytes 10485760 | tf_op jit(solution)/shard_map/reshape | solution.py:205
  220.4 16.0 %multiply_reduce_fusion = (f32[1024]{0:T(1024)S(1)}, f32[1024]{0:T(1024)S(1)}, f32[1024,1280]{1,0:T(8,128)}) fusion(f32[1280]{0:T(1024)S(1)} %copy-done.15, bf16[1024,2560]{1,0:T(8,128)(2,1)} %all-gather.8.cloned.1.call-done, bf16[2560,1280]{1,0:T(8,128)(2,1)} %param.18, bf16[1024,1280]{1,0:T(8,128)(2,1)} %bitcast.290, f32[1280]{0:T(1024)S(1)} %mul.413, ...), kind=kOutput, calls=%fused_computation.52 | convolution fusion | flops 6731855872 | bytes 30164992 | tf_op jit(solution)/shard_map/dot_general | solution.py:175
  237.0 4.4 %all-to-all-start = ((f32[4,2,1024]{2,1,0:T(2,128)}), f32[4,2,1024]{2,1,0:T(2,128)S(1)}, u32[]{:S(2)}, u32[]{:S(2)}) async-start(f32[4,2,1024]{2,1,0:T(2,128)} %broadcast_in_dim.33), calls=%async_computation | async-start | bytes 65536 | tf_op jit(solution)/shard_map/all_to_all | solution.py:51
  242.7 4.2 %all-to-all-done = f32[4,2,1024]{2,1,0:T(2,128)S(1)} async-done(((f32[4,2,1024]{2,1,0:T(2,128)}), f32[4,2,1024]{2,1,0:T(2,128)S(1)}, u32[]{:S(2)}, u32[]{:S(2)}) %all-to-all-start) | async-done | bytes 32800 | tf_op jit(solution)/shard_map/all_to_all | solution.py:51
  247.0 12.7 %convolution_convert_fusion = bf16[1024,2560]{1,0:T(8,128)(2,1)} fusion(bf16[1280,2560]{1,0:T(8,128)(2,1)} %param.30, f32[1024,1280]{1,0:T(8,128)} %get-tuple-element.174, f32[]{:T(128)S(6)} %div.31, f32[1024]{0:T(1024)S(1)} %bitcast.307, f32[1280]{0:T(1024)S(1)} %copy-done.15), kind=kOutput, calls=%fused_computation.43 | convolution fusion | flops 6720061440 | bytes 17048580 | tf_op jit(solution)/shard_map/dot_general | solution.py:219
  259.7 7.9 %copy.73 = bf16[1024,2560]{0,1:T(8,128)(2,1)} copy(bf16[1024,2560]{1,0:T(8,128)(2,1)} %convolution_convert_fusion) | data formatting | bytes 10485760
  269.1 13.5 %all_to_all.11 = f32[32,1,1]{2,1,0:T(1,128)S(1)} all-to-all(f32[32,1,1]{2,1,0:T(1,128)S(1)} %broadcast_in_dim.34), channel_id=1, replica_groups=mesh['seq_0'=4,'seq_1'=4,'seq_2'=2,'tp'=4] {'seq_0','seq_1','seq_2'}, dimensions={0} | all-to-all | bytes 256 | tf_op jit(solution)/shard_map/all_to_all | solution.py:51
  283.2 1.2 pad_maximum_fusion.3
  284.5 37.6 %reduce-scatter.4.cloned.1.call-done = bf16[640,1024]{1,0:T(8,128)(2,1)} async-done(((bf16[2560,1024]{1,0:T(8,128)(2,1)}), bf16[640,1024]{1,0:T(8,128)(2,1)}) %reduce-scatter.4.cloned.1.call-update) | async-done | bytes 1310736
  322.1 1.7 copy.74
  323.8 1.3 divide_convert_fusion
  (174 shorter events, 16.2 us)
Async XLA Ops:
  7.2 62.2 %copy-start = (bf16[2560,256]{1,0:T(8,128)(2,1)S(1)}, bf16[2560,256]{1,0:T(8,128)(2,1)}, u32[]{:S(2)}) copy-start(bf16[2560,256]{1,0:T(8,128)(2,1)} %param.20) | copy-start | bytes 3932164
  7.2 62.2 %all-gather.8.cloned.1.call-start = ((), (), s32[]{:S(2)}) async-start(), calls=%async_computation.3 | async-start | bytes 6553600 | tf_op jit(solution)/shard_map/all_gather | solution.py:173
  7.9 172.7 %all-gather.10.cloned.1.call-start = ((), (), s32[]{:S(2)}) async-start(), calls=%async_computation.4 | async-start | bytes 1638400 | tf_op jit(solution)/shard_map/all_gather | solution.py:34
  69.3 5.9 %copy-start.3 = (bf16[1024,2560]{1,0:T(8,128)(2,1)S(1)}, bf16[1024,2560]{1,0:T(8,128)(2,1)}, u32[]{:S(2)}) copy-start(bf16[1024,2560]{1,0:T(8,128)(2,1)} %all-gather.8.cloned.1.call-done) | copy-start | bytes 15728644
  73.5 15.8 %copy-start.10 = (bf16[2560,20]{0,1:T(8,128)(2,1)S(1)}, bf16[2560,20]{0,1:T(8,128)(2,1)}, u32[]{:S(2)}) copy-start(bf16[2560,20]{0,1:T(8,128)(2,1)} %param.21) | copy-start | bytes 307204
  73.5 15.8 %copy-start.12 = (f32[20]{0:T(128)S(1)}, f32[20]{0:T(128)}, u32[]{:S(2)}) copy-start(f32[20]{0:T(128)} %param.22) | copy-start | bytes 244
  73.5 22.3 %collective-permute-start.1 = (bf16[3,256]{1,0:T(4,128)(2,1)S(1)}, bf16[3,256]{1,0:T(4,128)(2,1)S(1)}, u32[]{:S(2)}, u32[]{:S(2)}) collective-permute-start(bf16[3,256]{1,0:T(4,128)(2,1)S(1)} %slice.240), channel_id=1, source_target_pairs={{0,4},{4,8},{8,12},{12,16},{16,20},{20,24},{24,28},{28,32},{32,36}... | collective-permute-start | bytes 4616 | tf_op jit(solution)/shard_map/ppermute | solution.py:19
  85.2 6.2 %copy-start.6 = (bf16[1024,1280]{1,0:T(8,128)(2,1)}, bf16[1024,1280]{1,0:T(8,128)(2,1)S(1)}, u32[]{:S(2)}) copy-start(bf16[1024,1280]{1,0:T(8,128)(2,1)S(1)} %convolution_convert_fusion.2) | copy-start | bytes 7864324
  85.3 10.5 %copy-start.13 = (f32[256]{0:T(256)S(1)}, f32[256]{0:T(256)}, u32[]{:S(2)}) copy-start(f32[256]{0:T(256)} %param.27) | copy-start | bytes 3076
  85.3 11.3 %copy-start.11 = (f32[1280]{0:T(1024)S(1)}, f32[1280]{0:T(1024)}, u32[]{:S(2)}) copy-start(f32[1280]{0:T(1024)} %param.25) | copy-start | bytes 15364
  85.3 11.3 %collective-permute-start = (bf16[3,1280]{1,0:T(4,128)(2,1)S(1)}, bf16[3,1280]{1,0:T(4,128)(2,1)S(1)}, u32[]{:S(2)}, u32[]{:S(2)}) collective-permute-start(bf16[3,1280]{1,0:T(4,128)(2,1)S(1)} %slice.235), channel_id=1, source_target_pairs={{0,4},{4,8},{8,12},{12,16},{16,20},{20,24},{24,28},{28,32},{32,36}... | collective-permute-start | bytes 23048 | tf_op jit(solution)/shard_map/ppermute | solution.py:19
  96.5 8.3 %copy-start.7 = (bf16[1024,256]{1,0:T(8,128)(2,1)}, bf16[1024,256]{1,0:T(8,128)(2,1)S(1)}, u32[]{:S(2)}) copy-start(bf16[1024,256]{1,0:T(8,128)(2,1)S(1)} %multiply_convert_fusion.5) | copy-start | bytes 1572868
  104.8 6.6 %copy-start.4 = (bf16[4,256,128]{2,1,0:T(8,128)(2,1)}, bf16[4,256,128]{2,1,0:T(8,128)(2,1)S(1)}, u32[]{:S(2)}) copy-start(bf16[4,256,128]{2,1,0:T(8,128)(2,1)S(1)} %get-tuple-element.260) | copy-start | bytes 786436 | tf_op jit(solution)/shard_map/while
  109.7 1.7 copy-start.2
  113.0 3.6 %copy-start.5 = (bf16[4,256,128]{2,1,0:T(8,128)(2,1)S(1)}, bf16[4,256,128]{2,1,0:T(8,128)(2,1)}, u32[]{:S(2)}) copy-start(bf16[4,256,128]{2,1,0:T(8,128)(2,1)} %copy-done.4) | copy-start | bytes 786436 | tf_op jit(solution)/shard_map/while
  116.6 6.6 %copy-start.4 = (bf16[4,256,128]{2,1,0:T(8,128)(2,1)}, bf16[4,256,128]{2,1,0:T(8,128)(2,1)S(1)}, u32[]{:S(2)}) copy-start(bf16[4,256,128]{2,1,0:T(8,128)(2,1)S(1)} %get-tuple-element.260) | copy-start | bytes 786436 | tf_op jit(solution)/shard_map/while
  121.5 1.7 copy-start.2
  124.8 3.6 %copy-start.5 = (bf16[4,256,128]{2,1,0:T(8,128)(2,1)S(1)}, bf16[4,256,128]{2,1,0:T(8,128)(2,1)}, u32[]{:S(2)}) copy-start(bf16[4,256,128]{2,1,0:T(8,128)(2,1)} %copy-done.4) | copy-start | bytes 786436 | tf_op jit(solution)/shard_map/while
  128.4 6.6 %copy-start.4 = (bf16[4,256,128]{2,1,0:T(8,128)(2,1)}, bf16[4,256,128]{2,1,0:T(8,128)(2,1)S(1)}, u32[]{:S(2)}) copy-start(bf16[4,256,128]{2,1,0:T(8,128)(2,1)S(1)} %get-tuple-element.260) | copy-start | bytes 786436 | tf_op jit(solution)/shard_map/while
  133.3 1.7 copy-start.2
  136.5 3.7 %copy-start.5 = (bf16[4,256,128]{2,1,0:T(8,128)(2,1)S(1)}, bf16[4,256,128]{2,1,0:T(8,128)(2,1)}, u32[]{:S(2)}) copy-start(bf16[4,256,128]{2,1,0:T(8,128)(2,1)} %copy-done.4) | copy-start | bytes 786436 | tf_op jit(solution)/shard_map/while
  140.2 6.6 %copy-start.4 = (bf16[4,256,128]{2,1,0:T(8,128)(2,1)}, bf16[4,256,128]{2,1,0:T(8,128)(2,1)S(1)}, u32[]{:S(2)}) copy-start(bf16[4,256,128]{2,1,0:T(8,128)(2,1)S(1)} %get-tuple-element.260) | copy-start | bytes 786436 | tf_op jit(solution)/shard_map/while
  145.1 1.7 copy-start.2
  148.4 3.6 %copy-start.5 = (bf16[4,256,128]{2,1,0:T(8,128)(2,1)S(1)}, bf16[4,256,128]{2,1,0:T(8,128)(2,1)}, u32[]{:S(2)}) copy-start(bf16[4,256,128]{2,1,0:T(8,128)(2,1)} %copy-done.4) | copy-start | bytes 786436 | tf_op jit(solution)/shard_map/while
  152.0 31.1 %copy-start.14 = (f32[20]{0:T(128)S(1)}, f32[20]{0:T(128)}, u32[]{:S(2)}) copy-start(f32[20]{0:T(128)} %param.28) | copy-start | bytes 244
  152.0 31.2 %copy-start.9 = (f32[20,1024]{1,0:T(8,128)S(1)}, f32[20,1024]{1,0:T(8,128)}, u32[]{:S(2)}) copy-start(f32[20,1024]{1,0:T(8,128)} %get-tuple-element.172) | copy-start | bytes 245764
  152.0 56.6 %copy-start.8 = (bf16[1024,256]{1,0:T(8,128)(2,1)S(1)}, bf16[1024,256]{1,0:T(8,128)(2,1)}, u32[]{:S(2)}) copy-start(bf16[1024,256]{1,0:T(8,128)(2,1)} %copy-done.7) | copy-start | bytes 1572868
  155.7 52.9 %all-gather.12.cloned.1.call-start = ((), (), s32[]{:S(2)}) async-start(), calls=%async_computation.5 | async-start | bytes 1638400 | tf_op jit(solution)/shard_map/all_gather | solution.py:34
  214.5 5.9 %copy-start.15 = (f32[1280]{0:T(1024)S(1)}, f32[1280]{0:T(1024)}, u32[]{:S(2)}) copy-start(f32[1280]{0:T(1024)} %param.29) | copy-start | bytes 15364
  220.4 21.1 %copy-start.16 = (f32[16]{0:T(128)S(1)}, f32[16]{0:T(128)}, u32[]{:S(2)}) copy-start(f32[16]{0:T(128)} %param.31) | copy-start | bytes 196
  237.0 9.9 %all-to-all-start = ((f32[4,2,1024]{2,1,0:T(2,128)}), f32[4,2,1024]{2,1,0:T(2,128)S(1)}, u32[]{:S(2)}, u32[]{:S(2)}) async-start(f32[4,2,1024]{2,1,0:T(2,128)} %broadcast_in_dim.33), calls=%async_computation | async-start | bytes 65536 | tf_op jit(solution)/shard_map/all_to_all | solution.py:51
  241.4 80.6 %reduce-scatter.4.cloned.1.call-start = ((), (), s32[]{:S(2)}) async-start(), calls=%async_computation.6 | async-start | bytes 6553600
  267.7 57.4 %copy-start.1 = (bf16[2560,256]{1,0:T(8,128)(2,1)S(1)}, bf16[2560,256]{1,0:T(8,128)(2,1)}, u32[]{:S(2)}) copy-start(bf16[2560,256]{1,0:T(8,128)(2,1)} %param.20) | copy-start | bytes 3932164
Sparse Core Ops, SparseCore 0:
  9.7 59.6 all-gather.7
  155.8 24.7 all-gather.9
  183.2 25.4 all-gather.11
  267.8 54.1 reduce-scatter.3
where the time goes:
time: 334 us; the launch traced here: 332 us
  waiting for transfers between devices  124 us (37%)
  matrix products  67.3 us (20%)
  local copies, waits for them, and re-layouts  38.3 us (11%)
  blocking collectives  38.1 us (11%)
  other arithmetic  37.7 us (11%)
  between operations  15.5 us (5%)
  starting transfers between devices  10.2 us (3%)
    all_gather x1, waiting for transfers between devices, shards(): piece = lax.all_gather(hidden, 'tp', axis=1, tiled=True)  57 us
    unnamed x5, waiting for transfers between devices  38.3 us
    dot_general x4, matrix products, shards(): jnp.dot(piece, matrix, preferred_element_type=jnp.float32)  32.3 us
    all_gather x2, waiting for transfers between devices, entering(): lax.all_gather(part.astype(kind), axis)  24.4 us
    all_gather x3, blocking collectives, entering(): lax.all_gather(part.astype(kind), axis)  22.2 us
    all_to_all x1, blocking collectives, from_everyone(): lax.all_to_all(jnp.broadcast_to(x[None], (size, *x.shape)), axis, 0, 0, t...  13.5 us
    dot_general x1, matrix products, shards(): partial_value = jnp.dot(quant, out_proj, preferred_element_type=jnp.float32)  12.7 us
    unnamed x38, local copies, waits for them, and re-layouts  11.3 us
  transfers between devices with their start and end apart: 7, of which 5 were waited for; matrix products, arithmetic and copies ran while one was open for 9% of the time, Pallas kernels for 0%

commit v1 on v0

v1 whole, which is shorter than its diff:
```python
import types

import jax
import jax.numpy as jnp
from jax import lax
from jax.experimental import pallas as pl
from jax.experimental.pallas import tpu as pltpu
from jax.sharding import PartitionSpec as P

QMAX = 448.0
EPS = 1e-05
HEAD = 64
LANES = 128
CHUNK = 128
RIM = 8
TAIL = 16
MESH = pl.DeviceIdType.MESH
F32 = jnp.float32
BF16 = jnp.bfloat16


def dot(a, b):
    return jnp.dot(a, b, preferred_element_type=F32)


def half_silu(v):
    half = 0.5 * v
    return half + half * jnp.tanh(half)


def softplus(v):
    u = jnp.exp(-jnp.abs(v))
    s = u / (2.0 + u)
    q = s * s
    series = jnp.full_like(q, 1.0 / 15.0)
    for k in (13, 11, 9, 7, 5, 3, 1):
        series = series * q + 1.0 / k
    return jnp.maximum(v, 0.0) + 2.0 * s * series


def conv_silu(window, weight, shift):
    total = shift + weight[3:4] * window[RIM:]
    for k in range(3):
        total = total + weight[k : k + 1] * pltpu.roll(window, 3 - k, 0)[RIM:]
    return half_silu(total)


def running_sum(lower, v):
    top = v.astype(BF16)
    rest = v - top.astype(F32)
    middle = rest.astype(BF16)
    last = (rest - middle.astype(F32)).astype(BF16)
    return dot(lower, top) + (dot(lower, middle) + dot(lower, last))


def pair_of(v, k, rows):
    low = lax.broadcasted_iota(jnp.int32, (rows, LANES), 1) < HEAD
    first = jnp.broadcast_to(v[:, 2 * k : 2 * k + 1], (rows, LANES))
    second = jnp.broadcast_to(v[:, 2 * k + 1 : 2 * k + 2], (rows, LANES))
    return first, second, jnp.where(low, first, second)


def build(rows, part, inner, n_tp, n_seq, heads):
    depth = part * n_tp
    pairs = heads // 2
    block = min(256, rows // 2)
    blocks = rows // block
    half = block // 2
    chunks = rows // CHUNK
    per = block // CHUNK
    slice_rows = max(8, LANES // n_seq)
    lane_parts = n_seq * slice_rows // LANES
    slice_lanes = inner // lane_parts
    ntile = 256

    vmem = {
        "h": ((rows, depth), BF16),
        "tail": ((TAIL, depth), BF16),
        "wg": ((depth, inner), BF16),
        "wx": ((depth, inner), BF16),
        "wb": ((depth, 2 * LANES), BF16),
        "ws": ((depth, LANES), BF16),
        "wo": ((inner, depth), BF16),
        "xp": ((rows + RIM, inner), F32),
        "bp": ((rows + RIM, 2 * LANES), F32),
        "sp": ((rows, LANES), F32),
        "gs": ((rows, inner), BF16),
        "ys": ((rows, inner), F32),
        "cs": ((rows, LANES), BF16),
        "cd": ((rows, LANES), F32),
        "yi": ((CHUNK, inner), F32),
        "xw": ((CHUNK, inner), BF16),
        "state": ((LANES, inner), F32),
        "dexp": ((1, inner), F32),
        "run": ((1, LANES), F32),
        "bias": ((1, LANES), F32),
        "rate": ((1, LANES), F32),
        "rimx": ((TAIL, inner), F32),
        "rimb": ((TAIL, 2 * LANES), F32),
        "stx": ((n_seq, slice_rows, slice_lanes), BF16),
        "srx": ((n_seq, slice_rows, slice_lanes), BF16),
        "ptx": ((n_seq, slice_rows, slice_lanes), BF16),
        "prx": ((n_seq, slice_rows, slice_lanes), BF16),
        "dtx": ((lane_parts, 1, slice_lanes), F32),
        "drx": ((n_seq, 1, slice_lanes), F32),
        "sin": ((LANES, inner), F32),
        "stat": ((n_tp, chunks, 8, LANES), F32),
        "tr": ((rows, part), BF16),
        "rl": ((rows // 2, part), BF16),
        "rr": ((rows // 2, part), BF16),
        "txp": ((rows, part), BF16),
        "txm": ((rows, part), BF16),
        "rxp": ((rows, part), BF16),
        "rxm": ((rows, part), BF16),
        "peak": ((1, LANES), F32),
        "pkt": ((1, LANES), F32),
        "pkr": ((n_seq, 1, LANES), F32),
    }
    dma = {
        "load": 7,
        "own_ps": blocks, "own_ms": blocks, "own_pr": blocks, "own_mr": blocks,
        "rel_ps": blocks, "rel_ms": blocks, "rel_pr": blocks, "rel_mr": blocks,
        "tail_s": n_tp, "tail_r": n_tp,
        "rim_s": 2, "rim_r": 2,
        "st_s": n_seq, "st_r": n_seq, "dc_s": n_seq, "dc_r": n_seq,
        "pf_s": n_seq, "pf_r": n_seq, "pk_s": n_seq, "pk_r": n_seq,
        "sa_s": chunks * n_tp, "sa_r": chunks * n_tp,
        "far_ps": blocks, "far_ms": blocks, "far_pr": blocks, "far_mr": blocks,
        "near_ps": blocks, "near_ms": blocks, "near_pr": blocks, "near_mr": blocks,
    }
    inputs = (
        "hidden", "gate_w", "in_w", "bc_w", "step_w", "step_b", "dlog", "conv_w", "conv_b",
        "bcc_w", "bcc_b", "skip", "gain", "out_w", "hist",
    )
    outputs = ("mixed", "news")
    names = (*inputs, *outputs, *vmem, *dma)

    def kernel(*refs):
        r = types.SimpleNamespace(**dict(zip(names, refs)))
        me = lax.axis_index("tp")
        at = lax.axis_index("seq")
        right = lax.rem(me + 1, n_tp)
        left = lax.rem(me + n_tp - 1, n_tp)
        opp = lax.rem(me + 2, n_tp)

        def cols(q):
            return pl.ds(pl.multiple_of(q * part, LANES), part)

        def brows(b):
            return pl.ds(pl.multiple_of(b * block, block), block)

        def hrows(b, side):
            return pl.ds(pl.multiple_of(b * block + side * half, half), half)

        def halfrows(b):
            return pl.ds(pl.multiple_of(b * half, half), half)

        def crows(k):
            return pl.ds(pl.multiple_of(k * CHUNK, CHUNK), CHUNK)

        def to_tp(src, dst, send, recv, q):
            return pltpu.make_async_remote_copy(
                src_ref=src, dst_ref=dst, send_sem=send, recv_sem=recv,
                device_id={"tp": q}, device_id_type=MESH,
            )

        def to_seq(src, dst, send, recv, q):
            return pltpu.make_async_remote_copy(
                src_ref=src, dst_ref=dst, send_sem=send, recv_sem=recv,
                device_id={"seq": q}, device_id_type=MESH,
            )

        loads = [
            pltpu.make_async_copy(src, dst, r.load.at[i])
            for i, (src, dst) in enumerate((
                (r.hidden, r.h.at[:, cols(me)]),
                (r.hidden.at[pl.ds(rows - TAIL, TAIL), :], r.tail.at[:, cols(me)]),
                (r.in_w, r.wx), (r.bc_w, r.wb), (r.gate_w, r.wg), (r.out_w, r.wo),
            ))
        ]
        for c in loads:
            c.start()

        barrier = pltpu.get_barrier_semaphore()
        for off in range(1, n_tp):
            pl.semaphore_signal(
                barrier, inc=1, device_id={"tp": lax.rem(me + off, n_tp)}, device_id_type=MESH
            )

        def greet(off, _):
            pl.semaphore_signal(
                barrier, inc=1, device_id={"seq": lax.rem(at + off, n_seq)}, device_id_type=MESH
            )
            return 0

        lax.fori_loop(1, n_seq, greet, 0)
        pl.semaphore_wait(barrier, n_tp - 1 + n_seq - 1)

        def own_p(b):
            here = r.h.at[brows(b), cols(me)]
            return to_tp(here, here, r.own_ps.at[b], r.own_pr.at[b], right)

        def own_m(b):
            here = r.h.at[brows(b), cols(me)]
            return to_tp(here, here, r.own_ms.at[b], r.own_mr.at[b], left)

        def rel_p(b):
            here = r.h.at[hrows(b, 0), cols(left)]
            return to_tp(here, here, r.rel_ps.at[b], r.rel_pr.at[b], right)

        def rel_m(b):
            here = r.h.at[hrows(b, 1), cols(right)]
            return to_tp(here, here, r.rel_ms.at[b], r.rel_mr.at[b], left)

        def got(view, sem):
            pltpu.make_async_copy(view, view, sem).wait()

        loads[1].wait()
        tails = []
        for off in range(1, n_tp):
            here = r.tail.at[:, cols(me)]
            tails.append(to_tp(
                here, here, r.tail_s.at[off], r.tail_r.at[off], lax.rem(me + off, n_tp)
            ))
            tails[-1].start()
        loads[0].wait()
        for b in range(2):
            own_p(b).start()
            own_m(b).start()

        r.ws[...] = jnp.zeros_like(r.ws)
        r.ws[:, :heads] = r.step_w[...]
        r.bias[...] = jnp.zeros_like(r.bias)
        r.bias[:, :heads] = r.step_b[...]
        r.rate[...] = jnp.zeros_like(r.rate)
        r.rate[:, :heads] = -jnp.exp(r.dlog[...])
        r.run[...] = jnp.zeros_like(r.run)
        r.state[...] = jnp.zeros_like(r.state)

        loads[2].wait()
        loads[3].wait()
        for off in range(1, n_tp):
            src = lax.rem(me + n_tp - off, n_tp)
            got(r.tail.at[:, cols(src)], r.tail_r.at[off])

        def rim_tile(n, _):
            lanes = pl.ds(pl.multiple_of(n * ntile, ntile), ntile)
            r.rimx[:, lanes] = dot(r.tail[...], r.wx[:, lanes])
            return 0

        lax.fori_loop(0, inner // ntile, rim_tile, 0)
        r.rimb[...] = dot(r.tail[...], r.wb[...])
        ahead = lax.rem(at + 1, n_seq)
        rims = (
            to_seq(r.rimx.at[pl.ds(TAIL - RIM, RIM), :], r.xp.at[pl.ds(0, RIM), :],
                   r.rim_s.at[0], r.rim_r.at[0], ahead),
            to_seq(r.rimb.at[pl.ds(TAIL - RIM, RIM), :], r.bp.at[pl.ds(0, RIM), :],
                   r.rim_s.at[1], r.rim_r.at[1], ahead),
        )

        @pl.when(at < n_seq - 1)
        def _():
            for c in rims:
                c.start()

        @pl.when(at == 0)
        def _():
            r.xp[0:RIM, :] = jnp.zeros((RIM, inner), F32)
            r.bp[0:RIM, :] = jnp.zeros((RIM, 2 * LANES), F32)

        def project(b):
            mine = brows(b)
            after = pl.ds(pl.multiple_of(b * block + RIM, 8), block)
            r.bp[after, :] = dot(r.h[mine, :], r.wb[...])
            r.sp[mine, :] = dot(r.h[mine, :], r.ws[...])

            def tile(n, _):
                lanes = pl.ds(pl.multiple_of(n * ntile, ntile), ntile)
                r.xp[after, lanes] = dot(r.h[mine, :], r.wx[:, lanes])
                return 0

            lax.fori_loop(0, inner // ntile, tile, 0)

        def project_gate(b):
            mine = brows(b)

            def tile(n, _):
                lanes = pl.ds(pl.multiple_of(n * ntile, ntile), ntile)
                r.gs[mine, lanes] = dot(r.h[mine, :], r.wg[:, lanes]).astype(BF16)
                return 0

            lax.fori_loop(0, inner // ntile, tile, 0)

        def recur(k):
            mine = crows(k)
            window = pl.ds(pl.multiple_of(k * CHUNK, CHUNK), CHUNK + RIM)
            bc = conv_silu(r.bp[window, :], r.bcc_w[...], r.bcc_b[...])
            b_t = bc[:, :LANES].T.astype(BF16)
            c_in = bc[:, LANES:].astype(BF16)
            r.cs[mine, :] = c_in
            down = lax.broadcasted_iota(jnp.int32, (CHUNK, CHUNK), 0)
            across = lax.broadcasted_iota(jnp.int32, (CHUNK, CHUNK), 1)
            causal = down >= across
            scores = jnp.where(causal, dot(c_in, b_t), 0.0)
            step = softplus(r.sp[mine, :] + r.bias[...])
            cum = running_sum(jnp.where(causal, 1.0, 0.0).astype(BF16), step * r.rate[...])
            cum_t = cum.T
            end = cum[CHUNK - 1 :, :]
            r.cd[mine, :] = cum + r.run[...]
            r.run[...] = r.run[...] + end
            r.yi[...] = dot(c_in, r.state[...].astype(BF16))
            low = lax.broadcasted_iota(jnp.int32, (CHUNK, LANES), 1) < HEAD
            for k2 in range(pairs):
                lanes = slice(k2 * LANES, (k2 + 1) * LANES)
                x = conv_silu(r.xp[window, lanes], r.conv_w[:, lanes], r.conv_b[:, lanes])
                first, second, both = pair_of(cum, k2, CHUNK)
                _, _, steps = pair_of(step, k2, CHUNK)
                last = both[CHUNK - 1 :, :]
                x_step = x * steps
                r.xw[:, lanes] = (jnp.exp(last - both) * x_step).astype(BF16)
                r.dexp[:, lanes] = jnp.exp(last)
                rise = [
                    (scores * jnp.exp(jnp.minimum(v - cum_t[2 * k2 + i : 2 * k2 + i + 1, :], 0.0)))
                    .astype(BF16)
                    for i, v in enumerate((first, second))
                ]
                fed = jnp.concatenate(
                    [jnp.where(low, x_step, 0.0), jnp.where(low, 0.0, x_step)], axis=0
                ).astype(BF16)
                _, _, kept = pair_of(r.skip[...], k2, 1)
                y = dot(jnp.concatenate(rise, axis=1), fed)
                r.ys[mine, lanes] = y + jnp.exp(both) * r.yi[:, lanes] + kept * x
            r.state[...] = r.dexp[...] * r.state[...] + dot(b_t, r.xw[...])

        def gather_step(b, _):
            @pl.when(b < blocks)
            def _():
                got(r.h.at[brows(b), cols(left)], r.own_pr.at[b])
                rel_p(b).start()
                got(r.h.at[brows(b), cols(right)], r.own_mr.at[b])
                rel_m(b).start()

                @pl.when(b + 2 < blocks)
                def _():
                    own_p(b + 2).start()
                    own_m(b + 2).start()

            @pl.when(b == 1)
            def _():
                @pl.when(at > 0)
                def _():
                    got(r.xp.at[pl.ds(0, RIM), :], r.rim_r.at[0])
                    got(r.bp.at[pl.ds(0, RIM), :], r.rim_r.at[1])

            @pl.when(b > 0)
            def _():
                done = b - 1
                got(r.h.at[hrows(done, 0), cols(opp)], r.rel_pr.at[done])
                got(r.h.at[hrows(done, 1), cols(opp)], r.rel_mr.at[done])
                project(done)
                lax.fori_loop(0, per, lambda j, _: (recur(done * per + j), 0)[1], 0)

            return 0

        lax.fori_loop(0, blocks + 1, gather_step, 0)

        for j in range(n_seq):
            top = (j // lane_parts) * slice_rows
            lane = (j % lane_parts) * slice_lanes
            r.stx[j] = r.state[top : top + slice_rows, lane : lane + slice_lanes].astype(BF16)
        for k2 in range(pairs):
            lanes = slice(k2 * LANES, (k2 + 1) * LANES)
            _, _, both = pair_of(r.run[...], k2, 1)
            r.dexp[:, lanes] = jnp.exp(both)
        for j in range(lane_parts):
            r.dtx[j] = r.dexp[:, j * slice_lanes : (j + 1) * slice_lanes]

        def state_to(off):
            q = lax.rem(at + off, n_seq)
            return (
                to_seq(r.stx.at[q], r.srx.at[at], r.st_s.at[off], r.st_r.at[off], q),
                to_seq(r.dtx.at[lax.rem(q, lane_parts)], r.drx.at[at],
                       r.dc_s.at[off], r.dc_r.at[off], q),
            )

        def state_send(off, _):
            for c in state_to(off):
                c.start()
            return 0

        lax.fori_loop(1, n_seq, state_send, 0)
        r.srx[at] = r.stx[at]
        r.drx[at] = r.dtx[lax.rem(at, lane_parts)]
        loads[4].wait()
        early = blocks // 2
        lax.fori_loop(0, early, lambda b, _: (project_gate(b), 0)[1], 0)

        def state_got(off, _):
            q = lax.rem(at + n_seq - off, n_seq)
            got(r.srx.at[q], r.st_r.at[off])
            got(r.drx.at[q], r.dc_r.at[off])
            return 0

        lax.fori_loop(1, n_seq, state_got, 0)

        def scan(j, before):
            r.ptx[j] = before.astype(BF16)
            return r.drx[j] * before + r.srx[j].astype(F32)

        lax.fori_loop(0, n_seq, scan, jnp.zeros((slice_rows, slice_lanes), F32))

        def prefix_to(off):
            q = lax.rem(at + off, n_seq)
            return to_seq(r.ptx.at[q], r.prx.at[at], r.pf_s.at[off], r.pf_r.at[off], q)

        def prefix_send(off, _):
            prefix_to(off).start()
            return 0

        lax.fori_loop(1, n_seq, prefix_send, 0)
        r.prx[at] = r.ptx[at]
        lax.fori_loop(early, blocks, lambda b, _: (project_gate(b), 0)[1], 0)

        def prefix_got(off, _):
            got(r.prx.at[lax.rem(at + n_seq - off, n_seq)], r.pf_r.at[off])
            return 0

        lax.fori_loop(1, n_seq, prefix_got, 0)
        for j in range(n_seq):
            top = (j // lane_parts) * slice_rows
            lane = (j % lane_parts) * slice_lanes
            r.sin[top : top + slice_rows, lane : lane + slice_lanes] = r.prx[j].astype(F32)

        def stat_to(k, off):
            here = r.stat.at[me, k]
            i = k * n_tp + off
            return to_tp(here, here, r.sa_s.at[i], r.sa_r.at[i], lax.rem(me + off, n_tp))

        def gate(k, _):
            mine = crows(k)
            r.yi[...] = dot(r.cs[mine, :], r.sin[...].astype(BF16))
            reach = r.cd[mine, :]
            squares = jnp.zeros((CHUNK, LANES), F32)
            tops = jnp.zeros((CHUNK, LANES), F32)
            for k2 in range(pairs):
                lanes = slice(k2 * LANES, (k2 + 1) * LANES)
                _, _, both = pair_of(reach, k2, CHUNK)
                out = r.ys[mine, lanes] + jnp.exp(both) * r.yi[:, lanes]
                gated = out * half_silu(r.gs[mine, lanes].astype(F32))
                squares = squares + gated * gated
                gained = gated * r.gain[:, lanes]
                tops = jnp.maximum(tops, jnp.abs(gained))
                r.ys[mine, lanes] = gained
            r.stat[me, k, 0:1, :] = jnp.sum(squares.T, axis=0, keepdims=True)
            r.stat[me, k, 1:2, :] = jnp.max(tops.T, axis=0, keepdims=True)
            for off in range(1, n_tp):
                stat_to(k, off).start()
            return 0

        lax.fori_loop(0, chunks, gate, 0)

        most = r.hist[0]
        for i in range(1, r.hist.shape[0]):
            most = jnp.maximum(most, r.hist[i])
        unscale = jnp.full((1, LANES), most, F32) / QMAX
        scale = QMAX / jnp.full((1, LANES), most, F32)
        r.peak[...] = jnp.zeros_like(r.peak)
        loads[5].wait()

        def norm(k):
            mine = crows(k)
            for off in range(1, n_tp):
                got(r.stat.at[lax.rem(me + n_tp - off, n_tp), k], r.sa_r.at[k * n_tp + off])
            squares = r.stat[0, k, 0:1, :]
            tops = r.stat[0, k, 1:2, :]
            for q in range(1, n_tp):
                squares = squares + r.stat[q, k, 0:1, :]
                tops = jnp.maximum(tops, r.stat[q, k, 1:2, :])
            inv = lax.rsqrt(squares * (1.0 / (inner * n_tp)) + EPS)
            r.peak[...] = jnp.maximum(r.peak[...], tops * inv)
            factor = jnp.broadcast_to(inv * scale, (CHUNK, LANES)).T
            for k2 in range(pairs):
                lanes = slice(k2 * LANES, (k2 + 1) * LANES)
                r.gs[mine, lanes] = jnp.clip(r.ys[mine, lanes] * factor, -QMAX, QMAX).astype(BF16)

        def far_p(b):
            return to_tp(r.tr.at[hrows(b, 0), :], r.rl.at[halfrows(b), :],
                         r.far_ps.at[b], r.far_pr.at[b], right)

        def far_m(b):
            return to_tp(r.tr.at[hrows(b, 1), :], r.rr.at[halfrows(b), :],
                         r.far_ms.at[b], r.far_mr.at[b], left)

        def near_p(b):
            return to_tp(r.txp.at[brows(b), :], r.rxp.at[brows(b), :],
                         r.near_ps.at[b], r.near_pr.at[b], right)

        def near_m(b):
            return to_tp(r.txm.at[brows(b), :], r.rxm.at[brows(b), :],
                         r.near_ms.at[b], r.near_mr.at[b], left)

        def far(b, _):
            lax.fori_loop(0, per, lambda j, _: (norm(b * per + j), 0)[1], 0)
            r.tr[brows(b), :] = dot(r.gs[brows(b), :], r.wo[:, cols(opp)]).astype(BF16)
            far_p(b).start()
            far_m(b).start()
            return 0

        lax.fori_loop(0, blocks, far, 0)
        r.pkt[...] = r.peak[...]

        def peak_to(off):
            q = lax.rem(at + off, n_seq)
            return to_seq(r.pkt, r.pkr.at[at], r.pk_s.at[off], r.pk_r.at[off], q)

        def peak_send(off, _):
            peak_to(off).start()
            return 0

        lax.fori_loop(1, n_seq, peak_send, 0)
        r.pkr[at] = r.peak[...]

        def near(b, _):
            mine = brows(b)
            r.txp[mine, :] = dot(r.gs[mine, :], r.wo[:, cols(right)]).astype(BF16)
            r.txm[mine, :] = dot(r.gs[mine, :], r.wo[:, cols(left)]).astype(BF16)
            got(r.rl.at[halfrows(b), :], r.far_pr.at[b])
            top = hrows(b, 0)
            r.txp[top, :] = (r.txp[top, :].astype(F32) + r.rl[halfrows(b), :].astype(F32)).astype(BF16)
            near_p(b).start()
            got(r.rr.at[halfrows(b), :], r.far_mr.at[b])
            low = hrows(b, 1)
            r.txm[low, :] = (r.txm[low, :].astype(F32) + r.rr[halfrows(b), :].astype(F32)).astype(BF16)
            near_m(b).start()
            return 0

        lax.fori_loop(0, blocks, near, 0)

        def finish(b, _):
            mine = brows(b)
            total = dot(r.gs[mine, :], r.wo[:, cols(me)])
            got(r.rxp.at[mine, :], r.near_pr.at[b])
            got(r.rxm.at[mine, :], r.near_mr.at[b])
            total = total + (r.rxp[mine, :].astype(F32) + r.rxm[mine, :].astype(F32))
            r.mixed[mine, :] = (total * unscale[0:1, 0:1]).astype(BF16)
            return 0

        lax.fori_loop(0, blocks, finish, 0)

        def peak_got(off, top):
            q = lax.rem(at + n_seq - off, n_seq)
            got(r.pkr.at[q], r.pk_r.at[off])
            return jnp.maximum(top, r.pkr[q])

        top = lax.fori_loop(1, n_seq, peak_got, r.pkr[at])
        r.news[0] = jnp.max(top)
        for i in range(1, r.hist.shape[0]):
            r.news[i] = r.hist[i - 1]

        for c in tails:
            c.wait_send()

        @pl.when(at < n_seq - 1)
        def _():
            for c in rims:
                c.wait_send()

        def sent_block(b, _):
            for make in (own_p, own_m, rel_p, rel_m, far_p, far_m, near_p, near_m):
                make(b).wait_send()
            return 0

        lax.fori_loop(0, blocks, sent_block, 0)

        def sent_seq(off, _):
            for c in (*state_to(off), prefix_to(off), peak_to(off)):
                c.wait_send()
            return 0

        lax.fori_loop(1, n_seq, sent_seq, 0)

        def sent_stat(k, _):
            for off in range(1, n_tp):
                stat_to(k, off).wait_send()
            return 0

        lax.fori_loop(0, chunks, sent_stat, 0)

    hbm = pl.BlockSpec(memory_space=pl.ANY)
    local = pl.BlockSpec(memory_space=pltpu.VMEM)
    scalars = pl.BlockSpec(memory_space=pltpu.SMEM)
    return pl.pallas_call(
        kernel,
        name="layer",
        out_shape=(
            jax.ShapeDtypeStruct((rows, part), BF16),
            jax.ShapeDtypeStruct((16,), F32),
        ),
        in_specs=[hbm] * 4 + [local] * 9 + [hbm, scalars],
        out_specs=(local, scalars),
        scratch_shapes=[pltpu.VMEM(*v) for v in vmem.values()]
        + [pltpu.SemaphoreType.DMA((n,)) for n in dma.values()],
        compiler_params=pltpu.CompilerParams(
            collective_id=0, has_side_effects=True, vmem_limit_bytes=67_043_328
        ),
    )


def solution(mesh):
    n_seq, n_tp = mesh.shape["seq"], mesh.shape["tp"]

    def shards(
        hidden, gate_proj, input_proj, bc_proj, step_proj, step_bias, decay_log, conv_weight,
        conv_bias, bc_conv_weight, bc_conv_bias, skip_gain, norm_gain, out_proj, amax_history,
    ):
        rows, part = hidden.shape
        call = build(rows, part, gate_proj.shape[1], n_tp, n_seq, step_proj.shape[1])
        return call(
            hidden, gate_proj, input_proj, bc_proj, step_proj, step_bias[None], decay_log[None],
            conv_weight, conv_bias[None], bc_conv_weight, bc_conv_bias[None], skip_gain[None],
            norm_gain[None], out_proj, amax_history,
        )

    cols = P(None, "tp")
    flat = P("tp")
    in_specs = (
        P("seq", "tp"), cols, cols, P(), cols, flat, flat, cols, flat, P(), P(), flat, flat,
        P("tp", None), P(),
    )
    return jax.shard_map(
        shards, mesh=mesh, in_specs=in_specs, out_specs=(P("seq", "tp"), P()), check_vma=False
    )
```

time: 334 us -> 144 us (0.43)
  Pallas kernels: 0 us -> 135 us
  waiting for transfers between devices: 124 us -> 0 us
  matrix products: 67.3 us -> 0 us
  blocking collectives: 38.1 us -> 0 us
  other arithmetic: 37.7 us -> 0 us
  local copies, waits for them, and re-layouts: 38.3 us -> 7.61 us
  between operations: 15.5 us -> 0.65 us
  starting transfers between devices: 10.2 us -> 0 us
    pallas_call x0 -> x1, Pallas kernels: none -> 135 us  [shards(): call(hidden, gate_proj, input_proj, bc_proj, step_proj, step_bias[None],...]
    all_gather x3 -> x0, waiting for transfers between devices: 81.4 us -> none  [the longest x1 57 us: shards(): piece = lax.all_gather(hidden, 'tp', axis=1, tiled=True)]
    dot_general x22 -> x0, matrix products: 67.3 us -> none  [the longest x4 32.3 us: shards(): jnp.dot(piece, matrix, preferred_element_type=jnp.float32)]
    unnamed x5 -> x0, waiting for transfers between devices: 38.3 us -> none
    all_gather x3 -> x0, blocking collectives: 22.2 us -> none  [entering(): lax.all_gather(part.astype(kind), axis)]
    convert_element_type x10 -> x0, other arithmetic: 18.6 us -> none  [the longest x2 8.95 us: conv_silu(): return jax.nn.silu(running + conv_shift).astype(jnp.bfloat16)]
    all_to_all x1 -> x0, blocking collectives: 13.5 us -> none  [from_everyone(): lax.all_to_all(jnp.broadcast_to(x[None], (size, *x.shape)), axis, 0, 0, t...]
    dynamic_slice x12 -> x0, local copies, waits for them, and re-layouts: 8.57 us -> none  [shards(): local_state, block_outs = lax.scan(ssd_block, zero_state, stacked)]
  transfers between devices with their start and end apart: 7 -> 0, of which waited for: 5 -> 0; matrix products, arithmetic and copies ran while one was open for 9% -> 0% of each run, Pallas kernels for 0% -> 0%
where the time goes in v1:
time: 144 us; the launch traced here: 143 us
  Pallas kernels  135 us (94%)
  local copies, waits for them, and re-layouts  7.61 us (5%)
    pallas_call x1, Pallas kernels, shards(): call(hidden, gate_proj, input_proj, bc_proj, step_proj, step_bias[None],...  135 us
    unnamed x5, local copies, waits for them, and re-layouts  5.03 us

profile of v1, /device:TPU:0, one launch (start us, length us, event | category | flops | bytes accessed | tf_op | source)
XLA Modules:
  0.0 143.3 jit_solution(15468303822278779504)
XLA Ops:
  0.6 1.3 broadcast_in_dim.20.refs_8_
  1.9 1.3 broadcast_in_dim.23.refs_12_
  3.2 2.0 %copy.17.refs_4_ = bf16[2560,20]{1,0:T(8,128)(2,1)} copy(bf16[2560,20]{0,1:T(8,128)(2,1)} %param.19) | data formatting | bytes 204800 | tf_op args[4]
  5.2 135.0 %layer.1 = (bf16[1024,640]{1,0:T(8,128)(2,1)}, f32[16]{0:T(128)}) custom-call(bf16[1024,640]{1,0:T(8,128)(2,1)} %refs_0_.1, bf16[2560,1280]{1,0:T(8,128)(2,1)} %refs_1_.1, bf16[2560,1280]{1,0:T(8,128)(2,1)} %refs_2_.1, bf16[2560,256]{1,0:T(8,128)(2,1)} %refs_3_.1, bf16[2560,20]{1,0:T(8,128)(2,1)} %copy.17.refs_4_, f32[1,20]{1,0:T(1,128)} %bitcast.5, ...), custom_call_target="tpu_custom_call" | custom-call | tf_op jit(solution)/shard_map/layer/pallas_call | solution.py:618
  140.3 0.0 copy-start
  140.3 2.5 %copy.20 = bf16[1024,640]{1,0:T(8,128)(2,1)} copy(bf16[1024,640]{1,0:T(8,128)(2,1)} %get-tuple-element.4) | data formatting | bytes 2621440
  142.8 0.0 copy-done
  142.8 0.5 copy.21
Async XLA Ops:
  140.3 2.5 %copy-start = (f32[16]{0:T(128)S(1)}, f32[16]{0:T(128)}, u32[]{:S(2)}) copy-start(f32[16]{0:T(128)} %get-tuple-element.5) | copy-start | bytes 196

commit v2 on v1

v2 whole, which is shorter than its diff:
```python
import types

import jax
import jax.numpy as jnp
from jax import lax
from jax.experimental import pallas as pl
from jax.experimental.pallas import tpu as pltpu
from jax.sharding import PartitionSpec as P

QMAX = 448.0
EPS = 1e-05
HEAD = 64
LANES = 128
CHUNK = 128
RIM = 8
TAIL = 16
MESH = pl.DeviceIdType.MESH
F32 = jnp.float32
BF16 = jnp.bfloat16


def dot(a, b):
    return jnp.dot(a, b, preferred_element_type=F32)


def half_silu(v):
    half = 0.5 * v
    return half + half * jnp.tanh(half)


def softplus(v):
    u = jnp.exp(-jnp.abs(v))
    s = u / (2.0 + u)
    q = s * s
    series = jnp.full_like(q, 1.0 / 15.0)
    for k in (13, 11, 9, 7, 5, 3, 1):
        series = series * q + 1.0 / k
    return jnp.maximum(v, 0.0) + 2.0 * s * series


def conv_silu(window, weight, shift):
    total = shift + weight[3:4] * window[RIM:]
    for k in range(3):
        total = total + weight[k : k + 1] * pltpu.roll(window, 3 - k, 0)[RIM:]
    return half_silu(total)


def running_sum(lower, v):
    top = v.astype(BF16)
    rest = v - top.astype(F32)
    middle = rest.astype(BF16)
    last = (rest - middle.astype(F32)).astype(BF16)
    return dot(lower, top) + (dot(lower, middle) + dot(lower, last))


def pair_of(v, k, rows):
    low = lax.broadcasted_iota(jnp.int32, (rows, LANES), 1) < HEAD
    first = jnp.broadcast_to(v[:, 2 * k : 2 * k + 1], (rows, LANES))
    second = jnp.broadcast_to(v[:, 2 * k + 1 : 2 * k + 2], (rows, LANES))
    return first, second, jnp.where(low, first, second)


def build(rows, part, inner, n_tp, n_seq, heads, split):
    depth = part * n_tp
    pairs = heads // 2
    block = min(256, rows // 2)
    blocks = rows // block
    half = block // 2
    chunks = rows // CHUNK
    per = block // CHUNK
    piece = 128
    pieces = rows // piece
    most_depth = 3 * part
    slice_rows = max(8, LANES // n_seq)
    lane_parts = n_seq * slice_rows // LANES
    slice_lanes = inner // lane_parts
    ntile = 256

    vmem = {
        "h": ((rows, depth), BF16),
        "tail": ((TAIL, depth), BF16),
        "wg": ((depth, inner), BF16),
        "wx": ((depth, inner), BF16),
        "wb": ((depth, 2 * LANES), BF16),
        "ws": ((LANES, depth), BF16),
        "wo": ((inner, depth), BF16),
        "xp": ((rows + RIM, inner), F32),
        "bp": ((rows + RIM, 2 * LANES), F32),
        "sp": ((rows, LANES), F32),
        "gs": ((rows, inner), BF16),
        "ys": ((rows, inner), F32),
        "cs": ((rows, LANES), BF16),
        "cd": ((rows, LANES), F32),
        "yi": ((CHUNK, inner), F32),
        "xw": ((CHUNK, inner), BF16),
        "xc": ((CHUNK, inner), BF16),
        "fed": ((2 * CHUNK, inner), BF16),
        "bt": ((LANES, CHUNK), BF16),
        "cum": ((CHUNK, LANES), F32),
        "state": ((LANES, inner), F32),
        "dexp": ((1, inner), F32),
        "run": ((1, LANES), F32),
        "bias": ((1, LANES), F32),
        "rate": ((1, LANES), F32),
        "rimx": ((TAIL, inner), F32),
        "rimb": ((TAIL, 2 * LANES), F32),
        "stx": ((n_seq, slice_rows, slice_lanes), BF16),
        "srx": ((n_seq, slice_rows, slice_lanes), BF16),
        "ptx": ((n_seq, slice_rows, slice_lanes), BF16),
        "prx": ((n_seq, slice_rows, slice_lanes), BF16),
        "dtx": ((lane_parts, 1, slice_lanes), F32),
        "drx": ((n_seq, 1, slice_lanes), F32),
        "sin": ((LANES, inner), F32),
        "stat": ((n_tp, chunks, 8, LANES), F32),
        "tr": ((rows, part), BF16),
        "rl": ((rows // 2, part), BF16),
        "rr": ((rows // 2, part), BF16),
        "txp": ((rows, part), BF16),
        "txm": ((rows, part), BF16),
        "rxp": ((rows, part), BF16),
        "rxm": ((rows, part), BF16),
        "peak": ((1, LANES), F32),
        "pkt": ((1, LANES), F32),
        "pkr": ((n_seq, 1, LANES), F32),
    }
    dma = {
        "load": 6,
        "own_ps": 1, "own_ms": 1, "own_pr": pieces, "own_mr": pieces,
        "rel_ps": 1, "rel_ms": 1, "rel_pr": pieces, "rel_mr": pieces,
        "tail_s": 1, "tail_r": 1, "rim_s": 2, "rim_r": 2,
        "st_s": 1, "st_r": 1, "dc_s": 1, "dc_r": 1,
        "pf_s": 1, "pf_r": 1, "pk_s": 1, "pk_r": 1,
        "sa_s": 1, "sa_r": chunks,
        "far_ps": 1, "far_ms": 1, "far_pr": chunks, "far_mr": chunks,
        "near_ps": 1, "near_ms": 1, "near_pr": blocks, "near_mr": blocks,
    }
    inputs = (
        "hidden", "gate_w", "in_w", "bc_w", "step_w", "step_b", "dlog", "conv_w", "conv_b",
        "bcc_w", "bcc_b", "skip", "gain", "out_w", "hist",
    )
    outputs = ("mixed", "news")
    names = (*inputs, *outputs, *vmem, *dma)

    def kernel(*refs):
        r = types.SimpleNamespace(**dict(zip(names, refs)))
        me = lax.axis_index("tp")
        at = lax.axis_index("seq")
        right = lax.rem(me + 1, n_tp)
        left = lax.rem(me + n_tp - 1, n_tp)
        opp = lax.rem(me + 2, n_tp)

        def cols(q):
            return pl.ds(pl.multiple_of(q * part, LANES), part)

        def brows(b):
            return pl.ds(pl.multiple_of(b * block, block), block)

        def hrows(b, side):
            return pl.ds(pl.multiple_of(b * block + side * half, half), half)

        def halfrows(b):
            return pl.ds(pl.multiple_of(b * half, half), half)

        def crows(k):
            return pl.ds(pl.multiple_of(k * CHUNK, CHUNK), CHUNK)

        def to_tp(src, dst, send, recv, q):
            return pltpu.make_async_remote_copy(
                src_ref=src, dst_ref=dst, send_sem=send, recv_sem=recv,
                device_id={"tp": q}, device_id_type=MESH,
            )

        def to_seq(src, dst, send, recv, q):
            return pltpu.make_async_remote_copy(
                src_ref=src, dst_ref=dst, send_sem=send, recv_sem=recv,
                device_id={"seq": q}, device_id_type=MESH,
            )

        slot = [slice(i * part, (i + 1) * part) for i in range(n_tp)]
        before, own, after, far_side = slot
        known = slice(0, most_depth)
        order = (left, me, right, opp)

        def load(src, dst, i):
            return pltpu.make_async_copy(src, dst, r.load.at[i])

        first = [
            load(r.hidden, r.h.at[:, own], 0),
            load(r.hidden.at[pl.ds(rows - TAIL, TAIL), :], r.tail.at[:, own], 1),
        ]
        for c in first:
            c.start()

        def by_rows(src, dst, i):
            return [
                load(src.at[pl.ds(pl.multiple_of(q * part, LANES), part), :],
                     dst.at[pl.ds(j * part, part), :], i)
                for j, q in enumerate(order)
            ]

        weights = (
            by_rows(r.in_w, r.wx, 2) + by_rows(r.bc_w, r.wb, 3) + by_rows(r.gate_w, r.wg, 4)
            + [load(r.out_w, r.wo, 5)]
        )

        barrier = pltpu.get_barrier_semaphore()
        for off in range(1, n_tp):
            pl.semaphore_signal(
                barrier, inc=1, device_id={"tp": lax.rem(me + off, n_tp)}, device_id_type=MESH
            )

        def greet(off, _):
            pl.semaphore_signal(
                barrier, inc=1, device_id={"seq": lax.rem(at + off, n_seq)}, device_id_type=MESH
            )
            return 0

        lax.fori_loop(1, n_seq, greet, 0)
        pl.semaphore_wait(barrier, n_tp - 1 + n_seq - 1)

        def prows(b):
            return pl.ds(pl.multiple_of(b * piece, piece), piece)

        def phalf(b, side):
            return pl.ds(pl.multiple_of(b * piece + side * (piece // 2), piece // 2), piece // 2)

        def own_p(b):
            return to_tp(r.h.at[prows(b), own], r.h.at[prows(b), before],
                         r.own_ps.at[0], r.own_pr.at[b], right)

        def own_m(b):
            return to_tp(r.h.at[prows(b), own], r.h.at[prows(b), after],
                         r.own_ms.at[0], r.own_mr.at[b], left)

        def rel_p(b):
            return to_tp(r.h.at[phalf(b, 0), before], r.h.at[phalf(b, 0), far_side],
                         r.rel_ps.at[0], r.rel_pr.at[b], right)

        def rel_m(b):
            return to_tp(r.h.at[phalf(b, 1), after], r.h.at[phalf(b, 1), far_side],
                         r.rel_ms.at[0], r.rel_mr.at[b], left)

        def got(view, sem):
            pltpu.make_async_copy(view, view, sem).wait()

        first[1].wait()
        tails = [
            to_tp(r.tail.at[:, own], r.tail.at[:, lanes], r.tail_s.at[0], r.tail_r.at[0], q)
            for lanes, q in ((before, right), (after, left), (far_side, opp))
        ]
        for c in tails:
            c.start()
        first[0].wait()
        for b in range(2):
            own_p(b).start()
            own_m(b).start()
        for c in weights:
            c.start()

        r.ws[...] = jnp.zeros_like(r.ws)
        for lanes, q in zip(slot, order):
            r.ws[:heads, lanes] = r.step_w[:, cols(q)]
        r.bias[...] = jnp.zeros_like(r.bias)
        r.bias[:, :heads] = r.step_b[...]
        r.rate[...] = jnp.zeros_like(r.rate)
        r.rate[:, :heads] = -jnp.exp(r.dlog[...])
        r.run[...] = jnp.zeros_like(r.run)
        r.state[...] = jnp.zeros_like(r.state)

        got(r.wx, r.load.at[2])
        got(r.wb, r.load.at[3])
        got(r.tail.at[:, known], r.tail_r.at[0])

        for n in range(inner // ntile):
            lanes = slice(n * ntile, (n + 1) * ntile)
            r.rimx[:, lanes] = dot(r.tail[...], r.wx[:, lanes])
        r.rimb[...] = dot(r.tail[...], r.wb[...])
        ahead = lax.rem(at + 1, n_seq)
        rims = (
            to_seq(r.rimx.at[pl.ds(TAIL - RIM, RIM), :], r.xp.at[pl.ds(0, RIM), :],
                   r.rim_s.at[0], r.rim_r.at[0], ahead),
            to_seq(r.rimb.at[pl.ds(TAIL - RIM, RIM), :], r.bp.at[pl.ds(0, RIM), :],
                   r.rim_s.at[1], r.rim_r.at[1], ahead),
        )

        @pl.when(at < n_seq - 1)
        def _():
            for c in rims:
                c.start()

        @pl.when(at == 0)
        def _():
            r.xp[0:RIM, :] = jnp.zeros((RIM, inner), F32)
            r.bp[0:RIM, :] = jnp.zeros((RIM, 2 * LANES), F32)

        def times_step(lanes, mine):
            return lax.dot_general(
                r.h[mine, lanes], r.ws[:, lanes], (((1,), (1,)), ((), ())),
                preferred_element_type=F32,
            )

        def project_known(b):
            mine = prows(b)
            later = pl.ds(pl.multiple_of(b * piece + RIM, 8), piece)
            r.bp[later, :] = dot(r.h[mine, known], r.wb[known, :])
            r.sp[mine, :] = times_step(known, mine)

            for n in range(inner // ntile):
                lanes = slice(n * ntile, (n + 1) * ntile)
                r.xp[later, lanes] = dot(r.h[mine, known], r.wx[known, lanes])

        def project_far(b):
            mine = prows(b)
            later = pl.ds(pl.multiple_of(b * piece + RIM, 8), piece)
            r.bp[later, :] = r.bp[later, :] + dot(r.h[mine, far_side], r.wb[far_side, :])
            r.sp[mine, :] = r.sp[mine, :] + times_step(far_side, mine)

            for n in range(inner // ntile):
                lanes = slice(n * ntile, (n + 1) * ntile)
                r.xp[later, lanes] = r.xp[later, lanes] + dot(
                    r.h[mine, far_side], r.wx[far_side, lanes]
                )

        def project_gate(b):
            mine = pl.ds(b * (rows // 2), rows // 2)
            for n in range(inner // ntile):
                lanes = slice(n * ntile, (n + 1) * ntile)
                r.gs[mine, lanes] = half_silu(dot(r.h[mine, :], r.wg[:, lanes])).astype(BF16)

        def conv_and_state(k):
            mine = crows(k)
            window = pl.ds(pl.multiple_of(k * CHUNK, CHUNK), CHUNK + RIM)
            bc = conv_silu(r.bp[window, :], r.bcc_w[...], r.bcc_b[...])
            b_t = bc[:, :LANES].T.astype(BF16)
            c_in = bc[:, LANES:].astype(BF16)
            r.bt[...] = b_t
            r.cs[mine, :] = c_in
            down = lax.broadcasted_iota(jnp.int32, (CHUNK, CHUNK), 0)
            across = lax.broadcasted_iota(jnp.int32, (CHUNK, CHUNK), 1)
            lower = jnp.where(down >= across, 1.0, 0.0).astype(BF16)
            step = softplus(r.sp[mine, :] + r.bias[...])
            cum = running_sum(lower, step * r.rate[...])
            end = cum[CHUNK - 1 :, :]
            rest = jnp.exp(end - cum) * step
            r.cum[...] = cum
            r.cd[mine, :] = cum + r.run[...]
            r.run[...] = r.run[...] + end
            r.yi[...] = dot(c_in, r.state[...].astype(BF16))
            low = lax.broadcasted_iota(jnp.int32, (CHUNK, LANES), 1) < HEAD
            ends = jnp.exp(end)
            for k2 in range(pairs):
                lanes = slice(k2 * LANES, (k2 + 1) * LANES)
                x = conv_silu(r.xp[window, lanes], r.conv_w[:, lanes], r.conv_b[k2 : k2 + 1, :])
                x_step = x * pair_of(step, k2, CHUNK)[2]
                r.xw[:, lanes] = (x * pair_of(rest, k2, CHUNK)[2]).astype(BF16)
                r.dexp[:, lanes] = pair_of(ends, k2, 1)[2]
                r.xc[:, lanes] = x.astype(BF16)
                r.fed[:CHUNK, lanes] = jnp.where(low, x_step, 0.0).astype(BF16)
                r.fed[CHUNK:, lanes] = jnp.where(low, 0.0, x_step).astype(BF16)
            r.state[...] = r.dexp[...] * r.state[...] + dot(b_t, r.xw[...])

        def within(k):
            mine = crows(k)
            down = lax.broadcasted_iota(jnp.int32, (CHUNK, CHUNK), 0)
            across = lax.broadcasted_iota(jnp.int32, (CHUNK, CHUNK), 1)
            scores = jnp.where(down >= across, dot(r.cs[mine, :], r.bt[...]), 0.0)
            cum = r.cum[...]
            cum_t = cum.T
            for k2 in range(pairs):
                lanes = slice(k2 * LANES, (k2 + 1) * LANES)
                first, second, both = pair_of(cum, k2, CHUNK)
                rise = [
                    (scores * jnp.exp(jnp.minimum(v - cum_t[2 * k2 + i : 2 * k2 + i + 1, :], 0.0)))
                    .astype(BF16)
                    for i, v in enumerate((first, second))
                ]
                kept = pair_of(r.skip[...], k2, 1)[2]
                y = dot(jnp.concatenate(rise, axis=1), r.fed[:, lanes])
                r.ys[mine, lanes] = (
                    y + jnp.exp(both) * r.yi[:, lanes] + kept * r.xc[:, lanes].astype(F32)
                )

        n_y, n_x, n_c = split
        y, x, core = at // (n_x * n_c), lax.rem(at // n_c, n_x), lax.rem(at, n_c)
        apart = sorted(
            ((dy, dx, dc) for dy in range(n_y) for dx in range(n_x) for dc in range(n_c)),
            key=lambda d: (-min(d[0], n_y - d[0]) - min(d[1], n_x - d[1]), -d[2]),
        )[:-1]

        def seq_of(d):
            py = lax.rem(y + d[0], n_y)
            px = lax.rem(x + d[1], n_x)
            return (py * n_x + px) * n_c + lax.rem(core + d[2], n_c)

        def send_states():
            for k2 in range(pairs):
                lanes = slice(k2 * LANES, (k2 + 1) * LANES)
                r.dexp[:, lanes] = jnp.exp(pair_of(r.run[...], k2, 1)[2])
            for j in range(lane_parts):
                r.dtx[j] = r.dexp[:, j * slice_lanes : (j + 1) * slice_lanes]
            for j in range(n_seq):
                top = (j // lane_parts) * slice_rows
                lane = (j % lane_parts) * slice_lanes
                r.stx[j] = r.state[top : top + slice_rows, lane : lane + slice_lanes].astype(BF16)
            for d in apart:
                q = seq_of(d)
                to_seq(r.dtx.at[lax.rem(q, lane_parts)], r.drx.at[at],
                       r.dc_s.at[0], r.dc_r.at[0], q).start()
                to_seq(r.stx.at[q], r.srx.at[at], r.st_s.at[0], r.st_r.at[0], q).start()

        def gather_step(b, _):
            @pl.when(b < pieces)
            def _():
                got(r.h.at[prows(b), before], r.own_pr.at[b])
                rel_p(b).start()
                got(r.h.at[prows(b), after], r.own_mr.at[b])
                rel_m(b).start()

                @pl.when(b + 2 < pieces)
                def _():
                    own_p(b + 2).start()
                    own_m(b + 2).start()

                project_known(b)

            @pl.when(b == 1)
            def _():
                @pl.when(at > 0)
                def _():
                    got(r.xp.at[pl.ds(0, RIM), :], r.rim_r.at[0])
                    got(r.bp.at[pl.ds(0, RIM), :], r.rim_r.at[1])

            @pl.when(b > 0)
            def _():
                done = b - 1
                got(r.h.at[phalf(done, 0), far_side], r.rel_pr.at[done])
                got(r.h.at[phalf(done, 1), far_side], r.rel_mr.at[done])
                project_far(done)
                conv_and_state(done)

                @pl.when(b == pieces)
                def _():
                    send_states()

                within(done)

            return 0

        lax.fori_loop(0, pieces + 1, gather_step, 0)
        r.srx[at] = r.stx[at]
        r.drx[at] = r.dtx[lax.rem(at, lane_parts)]
        others = pl.ds(0, n_seq - 1)
        got(r.wg, r.load.at[4])
        project_gate(0)
        got(r.drx.at[others], r.dc_r.at[0])
        got(r.srx.at[others], r.st_r.at[0])

        def scan(j, before):
            r.ptx[j] = before.astype(BF16)
            return r.drx[j] * before + r.srx[j].astype(F32)

        lax.fori_loop(0, n_seq, scan, jnp.zeros((slice_rows, slice_lanes), F32))

        for d in apart:
            q = seq_of(d)
            to_seq(r.ptx.at[q], r.prx.at[at], r.pf_s.at[0], r.pf_r.at[0], q).start()
        r.prx[at] = r.ptx[at]
        project_gate(1)
        got(r.prx.at[others], r.pf_r.at[0])
        for j in range(n_seq):
            top = (j // lane_parts) * slice_rows
            lane = (j % lane_parts) * slice_lanes
            r.sin[top : top + slice_rows, lane : lane + slice_lanes] = r.prx[j].astype(F32)

        def stat_to(k, off):
            here = r.stat.at[me, k]
            return to_tp(here, here, r.sa_s.at[0], r.sa_r.at[k], lax.rem(me + off, n_tp))

        def gate(k, _):
            mine = crows(k)
            r.yi[...] = dot(r.cs[mine, :], r.sin[...].astype(BF16))
            reach = r.cd[mine, :]
            squares = jnp.zeros((CHUNK, LANES), F32)
            tops = jnp.zeros((CHUNK, LANES), F32)
            for k2 in range(pairs):
                lanes = slice(k2 * LANES, (k2 + 1) * LANES)
                _, _, both = pair_of(reach, k2, CHUNK)
                out = r.ys[mine, lanes] + jnp.exp(both) * r.yi[:, lanes]
                gated = out * r.gs[mine, lanes].astype(F32)
                squares = squares + gated * gated
                gained = gated * r.gain[k2 : k2 + 1, :]
                tops = jnp.maximum(tops, jnp.abs(gained))
                r.ys[mine, lanes] = gained
            r.stat[me, k, 0:1, :] = jnp.sum(squares.T, axis=0, keepdims=True)
            r.stat[me, k, 1:2, :] = jnp.max(tops.T, axis=0, keepdims=True)
            for off in range(1, n_tp):
                stat_to(k, off).start()
            return 0

        most = r.hist[0]
        for i in range(1, r.hist.shape[0]):
            most = jnp.maximum(most, r.hist[i])
        unscale = jnp.full((1, LANES), most, F32) / QMAX
        scale = QMAX / jnp.full((1, LANES), most, F32)
        r.peak[...] = jnp.zeros_like(r.peak)
        got(r.wo, r.load.at[5])

        def norm(k):
            mine = crows(k)
            got(r.stat.at[pl.ds(0, n_tp - 1), k], r.sa_r.at[k])
            squares = r.stat[0, k, 0:1, :]
            tops = r.stat[0, k, 1:2, :]
            for q in range(1, n_tp):
                squares = squares + r.stat[q, k, 0:1, :]
                tops = jnp.maximum(tops, r.stat[q, k, 1:2, :])
            inv = lax.rsqrt(squares * (1.0 / (inner * n_tp)) + EPS)
            r.peak[...] = jnp.maximum(r.peak[...], tops * inv)
            factor = jnp.broadcast_to(inv * scale, (CHUNK, LANES)).T
            for k2 in range(pairs):
                lanes = slice(k2 * LANES, (k2 + 1) * LANES)
                r.gs[mine, lanes] = jnp.clip(r.ys[mine, lanes] * factor, -QMAX, QMAX).astype(BF16)

        def khalf(k, side):
            return pl.ds(pl.multiple_of(k * CHUNK + side * (CHUNK // 2), CHUNK // 2), CHUNK // 2)

        def kept_half(k):
            return pl.ds(pl.multiple_of(k * (CHUNK // 2), CHUNK // 2), CHUNK // 2)

        def far_p(k):
            return to_tp(r.tr.at[khalf(k, 0), :], r.rl.at[kept_half(k), :],
                         r.far_ps.at[0], r.far_pr.at[k], right)

        def far_m(k):
            return to_tp(r.tr.at[khalf(k, 1), :], r.rr.at[kept_half(k), :],
                         r.far_ms.at[0], r.far_mr.at[k], left)

        def near_p(b):
            return to_tp(r.txp.at[brows(b), :], r.rxp.at[brows(b), :],
                         r.near_ps.at[0], r.near_pr.at[b], right)

        def near_m(b):
            return to_tp(r.txm.at[brows(b), :], r.rxm.at[brows(b), :],
                         r.near_ms.at[0], r.near_mr.at[b], left)

        lag = min(4, chunks)

        def far(k, _):
            @pl.when(k < chunks)
            def _():
                gate(k, 0)

            @pl.when(k >= lag)
            def _():
                ready = k - lag
                norm(ready)
                mine = crows(ready)
                r.tr[mine, :] = dot(r.gs[mine, :], r.wo[:, cols(opp)]).astype(BF16)
                far_p(ready).start()
                far_m(ready).start()

            return 0

        lax.fori_loop(0, chunks + lag, far, 0)
        r.pkt[...] = r.peak[...]

        def peak_to(off):
            q = lax.rem(at + off, n_seq)
            return to_seq(r.pkt, r.pkr.at[at], r.pk_s.at[0], r.pk_r.at[0], q)

        def peak_send(off, _):
            peak_to(off).start()
            return 0

        lax.fori_loop(1, n_seq, peak_send, 0)
        r.pkr[at] = r.peak[...]

        def near(b, _):
            mine = brows(b)
            r.txp[mine, :] = dot(r.gs[mine, :], r.wo[:, cols(right)]).astype(BF16)
            r.txm[mine, :] = dot(r.gs[mine, :], r.wo[:, cols(left)]).astype(BF16)
            for j in range(per):
                k = b * per + j
                top = khalf(k, 0)
                got(r.rl.at[kept_half(k), :], r.far_pr.at[k])
                r.txp[top, :] = (
                    r.txp[top, :].astype(F32) + r.rl[kept_half(k), :].astype(F32)
                ).astype(BF16)
            near_p(b).start()
            for j in range(per):
                k = b * per + j
                low = khalf(k, 1)
                got(r.rr.at[kept_half(k), :], r.far_mr.at[k])
                r.txm[low, :] = (
                    r.txm[low, :].astype(F32) + r.rr[kept_half(k), :].astype(F32)
                ).astype(BF16)
            near_m(b).start()
            return 0

        lax.fori_loop(0, blocks, near, 0)

        def finish(b, _):
            mine = brows(b)
            total = dot(r.gs[mine, :], r.wo[:, cols(me)])
            got(r.rxp.at[mine, :], r.near_pr.at[b])
            got(r.rxm.at[mine, :], r.near_mr.at[b])
            total = total + (r.rxp[mine, :].astype(F32) + r.rxm[mine, :].astype(F32))
            r.mixed[mine, :] = (total * unscale[0:1, 0:1]).astype(BF16)
            return 0

        lax.fori_loop(0, blocks, finish, 0)

        got(r.pkr.at[others], r.pk_r.at[0])
        top = lax.fori_loop(0, n_seq, lambda j, v: jnp.maximum(v, r.pkr[j]), r.peak[...])
        lane = lax.broadcasted_iota(jnp.int32, r.news.shape, 1)
        news = jnp.broadcast_to(jnp.max(top, axis=1, keepdims=True), r.news.shape)
        for i in range(1, r.hist.shape[0]):
            news = jnp.where(lane == i, r.hist[i - 1], news)
        r.news[...] = news

        got(r.tail.at[:, known], r.tail_s.at[0])

        @pl.when(at < n_seq - 1)
        def _():
            for c in rims:
                c.wait_send()

        half_own = r.h.at[pl.ds(0, rows // 2), own]
        for view, sem in (
            (r.h.at[:, own], r.own_ps), (r.h.at[:, own], r.own_ms),
            (half_own, r.rel_ps), (half_own, r.rel_ms),
            (r.rl, r.far_ps), (r.rr, r.far_ms), (r.txp, r.near_ps), (r.txm, r.near_ms),
            (r.drx.at[others], r.dc_s), (r.srx.at[others], r.st_s),
            (r.prx.at[others], r.pf_s), (r.pkr.at[others], r.pk_s),
            (r.stat.at[pl.ds(0, n_tp - 1)], r.sa_s),
        ):
            got(view, sem.at[0])

    hbm = pl.BlockSpec(memory_space=pl.ANY)
    local = pl.BlockSpec(memory_space=pltpu.VMEM)
    scalars = pl.BlockSpec(memory_space=pltpu.SMEM)
    return pl.pallas_call(
        kernel,
        name="layer",
        out_shape=(
            pltpu.VMEM((rows, part), BF16),
            pltpu.VMEM((1, 16), F32),
        ),
        in_specs=[hbm] * 4 + [local] * 9 + [hbm, scalars],
        out_specs=(local, local),
        scratch_shapes=[pltpu.VMEM(*v) for v in vmem.values()]
        + [pltpu.SemaphoreType.DMA((n,)) for n in dma.values()],
        compiler_params=pltpu.CompilerParams(
            collective_id=0, has_side_effects=True, vmem_limit_bytes=65_650_000
        ),
    )


def solution(mesh):
    n_seq, n_tp = mesh.shape["seq"], mesh.shape["tp"]
    side = max(k for k in range(1, n_seq) if 2 * k * k <= n_seq and n_seq % (2 * k) == 0)
    split = (n_seq // (2 * side), side, 2)

    def shards(
        hidden, gate_proj, input_proj, bc_proj, step_proj, step_bias, decay_log, conv_weight,
        conv_bias, bc_conv_weight, bc_conv_bias, skip_gain, norm_gain, out_proj, amax_history,
    ):
        rows, part = hidden.shape
        call = build(rows, part, gate_proj.shape[1], n_tp, n_seq, step_proj.shape[1], split)
        mixed, news = call(
            hidden, gate_proj, input_proj, bc_proj, step_proj.T, step_bias[None], decay_log[None],
            conv_weight, conv_bias.reshape(-1, LANES), bc_conv_weight, bc_conv_bias[None],
            skip_gain[None], norm_gain.reshape(-1, LANES), out_proj, amax_history,
        )
        return mixed, news.reshape(-1)

    cols = P(None, "tp")
    flat = P("tp")
    in_specs = (
        P("seq", "tp"), cols, cols, P(), cols, flat, flat, cols, flat, P(), P(), flat, flat,
        P("tp", None), P(),
    )
    return jax.shard_map(
        shards, mesh=mesh, in_specs=in_specs, out_specs=(P("seq", "tp"), P()), check_vma=False
    )
```

time: 144 us -> 124 us (0.86)
  Pallas kernels: 135 us -> 122 us
  local copies, waits for them, and re-layouts: 7.61 us -> 1.57 us
    pallas_call x1, Pallas kernels: 135 us -> 122 us  [shards(): call(hidden, gate_proj, input_proj, bc_proj, step_proj.T, step_bias[None]...]
    unnamed x5 -> x2, local copies, waits for them, and re-layouts: 5.03 us -> 1.57 us
    broadcast_in_dim x2 -> x0, local copies, waits for them, and re-layouts: 2.59 us -> none  [the longest x1 1.29 us: shards(): norm_gain[None]]
where the time goes in v2:
time: 124 us
  Pallas kernels  122 us (98%)
  local copies, waits for them, and re-layouts  1.57 us (1%)
    pallas_call x1, Pallas kernels, shards(): call(hidden, gate_proj, input_proj, bc_proj, step_proj.T, step_bias[None]...  122 us

profile of v2, /device:TPU:0, one launch (start us, length us, event | category | flops | bytes accessed | tf_op | source)
XLA Modules:
  0.0 123.9 jit_solution(3262439462537701148)
XLA Ops:
  0.6 121.7 %layer.1 = (bf16[1024,640]{1,0:T(8,128)(2,1)S(1)}, f32[1,16]{1,0:T(1,128)S(1)}) custom-call(bf16[1024,640]{1,0:T(8,128)(2,1)} %refs_0_.1, bf16[2560,1280]{1,0:T(8,128)(2,1)} %refs_1_.1, bf16[2560,1280]{1,0:T(8,128)(2,1)} %refs_2_.1, bf16[2560,256]{1,0:T(8,128)(2,1)} %refs_3_.1, bf16[20,2560]{1,0:T(8,128)(2,1)} %bitcast.9, f32[1,20]{1,0:T(1,128)} %bitcast.13, ...), custom_call_target="tpu_custom_call" | custom-call | tf_op jit(solution)/shard_map/layer/pallas_call | solution.py:669
  122.3 1.1 copy.19
  123.4 0.5 copy.20

commit v3 on v2

--- a/solution.py
+++ b/solution.py
@@ -63,7 +63,7 @@
 def build(rows, part, inner, n_tp, n_seq, heads, split):
     depth = part * n_tp
     pairs = heads // 2
-    block = min(256, rows // 2)
+    block = 256
     blocks = rows // block
     half = block // 2
     chunks = rows // CHUNK
@@ -71,6 +71,15 @@
     piece = 128
     pieces = rows // piece
     most_depth = 3 * part
+    half_rows = rows // 2
+    hp = pieces // 2
+    scan_at = min(pieces, hp + 3)
+    hc = chunks // 2
+    half_blocks = blocks // 2
+    n_y, n_x, n_c = split
+    wide = n_x * n_c
+    first_near = hc - 1
+    held = max(first_near - 2, 0)
     slice_rows = max(8, LANES // n_seq)
     lane_parts = n_seq * slice_rows // LANES
     slice_lanes = inner // lane_parts
@@ -78,14 +87,17 @@
 
     vmem = {
         "h": ((rows, depth), BF16),
-        "tail": ((TAIL, depth), BF16),
+        "tail": ((2 * TAIL, depth), BF16),
+        "swap": ((rows // 2, part), BF16),
+        "otx": ((rows // 2, part), BF16),
+        "orx": ((rows // 2, part), BF16),
         "wg": ((depth, inner), BF16),
         "wx": ((depth, inner), BF16),
         "wb": ((depth, 2 * LANES), BF16),
         "ws": ((LANES, depth), BF16),
         "wo": ((inner, depth), BF16),
-        "xp": ((rows + RIM, inner), F32),
-        "bp": ((rows + RIM, 2 * LANES), F32),
+        "xp": ((rows + 2 * RIM, inner), F32),
+        "bp": ((rows + 2 * RIM, 2 * LANES), F32),
         "sp": ((rows, LANES), F32),
         "gs": ((rows, inner), BF16),
         "ys": ((rows, inner), F32),
@@ -93,23 +105,23 @@
         "cd": ((rows, LANES), F32),
         "yi": ((CHUNK, inner), F32),
         "xw": ((CHUNK, inner), BF16),
+        "yg": ((CHUNK, inner), F32),
         "xc": ((CHUNK, inner), BF16),
         "fed": ((2 * CHUNK, inner), BF16),
         "bt": ((LANES, CHUNK), BF16),
         "cum": ((CHUNK, LANES), F32),
-        "state": ((LANES, inner), F32),
+        "state": ((2, LANES, inner), F32),
         "dexp": ((1, inner), F32),
-        "run": ((1, LANES), F32),
+        "run": ((2, 1, LANES), F32),
+        "carry": ((slice_rows, slice_lanes), F32),
         "bias": ((1, LANES), F32),
         "rate": ((1, LANES), F32),
-        "rimx": ((TAIL, inner), F32),
-        "rimb": ((TAIL, 2 * LANES), F32),
-        "stx": ((n_seq, slice_rows, slice_lanes), BF16),
-        "srx": ((n_seq, slice_rows, slice_lanes), BF16),
-        "ptx": ((n_seq, slice_rows, slice_lanes), BF16),
-        "prx": ((n_seq, slice_rows, slice_lanes), BF16),
-        "dtx": ((lane_parts, 1, slice_lanes), F32),
-        "drx": ((n_seq, 1, slice_lanes), F32),
+        "stx": ((2, n_seq, slice_rows, slice_lanes), BF16),
+        "srx": ((2, n_seq, slice_rows, slice_lanes), BF16),
+        "ptx": ((2, n_seq, slice_rows, slice_lanes), BF16),
+        "prx": ((2, n_seq, slice_rows, slice_lanes), BF16),
+        "dtx": ((2, lane_parts, 1, slice_lanes), F32),
+        "drx": ((2, n_seq, 1, slice_lanes), F32),
         "sin": ((LANES, inner), F32),
         "stat": ((n_tp, chunks, 8, LANES), F32),
         "tr": ((rows, part), BF16),
@@ -123,23 +135,35 @@
         "pkt": ((1, LANES), F32),
         "pkr": ((n_seq, 1, LANES), F32),
     }
+    small = {
+        "step_w": ((heads, depth), BF16),
+        "step_b": ((1, heads), F32),
+        "dlog": ((1, heads), F32),
+        "conv_w": ((4, inner), F32),
+        "conv_b": ((inner // LANES, LANES), F32),
+        "bcc_w": ((4, 2 * LANES), F32),
+        "bcc_b": ((1, 2 * LANES), F32),
+        "skip": ((1, heads), F32),
+        "gain": ((inner // LANES, LANES), F32),
+    }
     dma = {
+        "smalls": len(small),
         "load": 6,
         "own_ps": 1, "own_ms": 1, "own_pr": pieces, "own_mr": pieces,
         "rel_ps": 1, "rel_ms": 1, "rel_pr": pieces, "rel_mr": pieces,
         "tail_s": 1, "tail_r": 1, "rim_s": 2, "rim_r": 2,
-        "st_s": 1, "st_r": 1, "dc_s": 1, "dc_r": 1,
-        "pf_s": 1, "pf_r": 1, "pk_s": 1, "pk_r": 1,
+        "swap_s": 1, "swap_r": hp, "out_s": 1, "out_r": hc,
+        "st_s": 2, "st_r": 2, "dc_s": 2, "dc_r": 2,
+        "pf_s": 2, "pf_r": 2, "pk_s": 1, "pk_r": 1,
         "sa_s": 1, "sa_r": chunks,
         "far_ps": 1, "far_ms": 1, "far_pr": chunks, "far_mr": chunks,
-        "near_ps": 1, "near_ms": 1, "near_pr": blocks, "near_mr": blocks,
+        "near_ps": 1, "near_ms": 1, "near_pr": chunks, "near_mr": chunks,
     }
     inputs = (
-        "hidden", "gate_w", "in_w", "bc_w", "step_w", "step_b", "dlog", "conv_w", "conv_b",
-        "bcc_w", "bcc_b", "skip", "gain", "out_w", "hist",
+        "hidden", "gate_w", "in_w", "bc_w", *(k + "_in" for k in small), "out_w", "hist",
     )
     outputs = ("mixed", "news")
-    names = (*inputs, *outputs, *vmem, *dma)
+    names = (*inputs, *outputs, *vmem, *small, *dma)
 
     def kernel(*refs):
         r = types.SimpleNamespace(**dict(zip(names, refs)))
@@ -148,18 +172,19 @@
         right = lax.rem(me + 1, n_tp)
         left = lax.rem(me + n_tp - 1, n_tp)
         opp = lax.rem(me + 2, n_tp)
+        late = at // (n_seq // 2)
+
+        def mate_of(q):
+            return (n_y - 1 - q // wide) * wide + lax.rem(q, wide)
+
+        mate = mate_of(at)
+        home = pl.multiple_of(late * half_rows, half_rows)
 
         def cols(q):
             return pl.ds(pl.multiple_of(q * part, LANES), part)
 
         def brows(b):
             return pl.ds(pl.multiple_of(b * block, block), block)
-
-        def hrows(b, side):
-            return pl.ds(pl.multiple_of(b * block + side * half, half), half)
-
-        def halfrows(b):
-            return pl.ds(pl.multiple_of(b * half, half), half)
 
         def crows(k):
             return pl.ds(pl.multiple_of(k * CHUNK, CHUNK), CHUNK)
@@ -185,8 +210,8 @@
             return pltpu.make_async_copy(src, dst, r.load.at[i])
 
         first = [
-            load(r.hidden, r.h.at[:, own], 0),
-            load(r.hidden.at[pl.ds(rows - TAIL, TAIL), :], r.tail.at[:, own], 1),
+            load(r.hidden.at[pl.ds(0, half_rows), :], r.h.at[pl.ds(home, half_rows), own], 0),
+            load(r.hidden.at[pl.ds(half_rows, half_rows), :], r.swap, 1),
         ]
         for c in first:
             c.start()
@@ -203,6 +228,11 @@
             + [load(r.out_w, r.wo, 5)]
         )
 
+        smalls = [
+            pltpu.make_async_copy(getattr(r, k + "_in"), getattr(r, k), r.smalls.at[i])
+            for i, k in enumerate(small)
+        ]
+
         barrier = pltpu.get_barrier_semaphore()
         for off in range(1, n_tp):
             pl.semaphore_signal(
@@ -243,19 +273,57 @@
         def got(view, sem):
             pltpu.make_async_copy(view, view, sem).wait()
 
-        first[1].wait()
-        tails = [
-            to_tp(r.tail.at[:, own], r.tail.at[:, lanes], r.tail_s.at[0], r.tail_r.at[0], q)
-            for lanes, q in ((before, right), (after, left), (far_side, opp))
-        ]
-        for c in tails:
-            c.start()
-        first[0].wait()
-        for b in range(2):
+        def place(i):
+            zero = (pieces - i) // pieces
+            low = (hp - i + pieces) // pieces
+            return i + late * (zero * hp - (low - zero))
+
+        def send_own(i):
+            b = place(i)
+
+            @pl.when(b // hp != late)
+            def _():
+                got(r.h.at[prows(b), own], r.swap_r.at[lax.rem(b, hp)])
+
             own_p(b).start()
             own_m(b).start()
-        for c in weights:
+
+        def swap(j):
+            here = pl.ds(j * piece, piece)
+            there = pl.ds(pl.multiple_of(late * half_rows + j * piece, piece), piece)
+            return to_seq(r.swap.at[here, :], r.h.at[there, own],
+                          r.swap_s.at[0], r.swap_r.at[j], mate)
+
+        ahead = lax.rem(at + 1, n_seq)
+        theirs = (ahead // (n_seq // 2)) * TAIL
+        rims = (
+            to_seq(r.swap.at[pl.ds(half_rows - TAIL, TAIL), :],
+                   r.tail.at[pl.ds(pl.multiple_of(theirs, TAIL), TAIL), own],
+                   r.rim_s.at[0], r.rim_r.at[0], ahead),
+            to_seq(r.h.at[pl.ds(pl.multiple_of(home + half_rows - TAIL, TAIL), TAIL), own],
+                   r.tail.at[pl.ds(pl.multiple_of(late * TAIL, TAIL), TAIL), own],
+                   r.rim_s.at[1], r.rim_r.at[1], mate),
+        )
+        first[1].wait()
+
+        @pl.when(at < n_seq - 1)
+        def _():
+            rims[0].start()
+
+        first[0].wait()
+        rims[1].start()
+        send_own(0)
+
+        @pl.when(late == 0)
+        def _():
+            send_own(1)
+
+        for j in range(hp):
+            swap(j).start()
+        for c in (*smalls, *weights):
             c.start()
+        for c in smalls:
+            c.wait()
 
         r.ws[...] = jnp.zeros_like(r.ws)
         for lanes, q in zip(slot, order):
@@ -266,32 +334,38 @@
         r.rate[:, :heads] = -jnp.exp(r.dlog[...])
         r.run[...] = jnp.zeros_like(r.run)
         r.state[...] = jnp.zeros_like(r.state)
-
-        got(r.wx, r.load.at[2])
-        got(r.wb, r.load.at[3])
-        got(r.tail.at[:, known], r.tail_r.at[0])
-
-        for n in range(inner // ntile):
-            lanes = slice(n * ntile, (n + 1) * ntile)
-            r.rimx[:, lanes] = dot(r.tail[...], r.wx[:, lanes])
-        r.rimb[...] = dot(r.tail[...], r.wb[...])
-        ahead = lax.rem(at + 1, n_seq)
-        rims = (
-            to_seq(r.rimx.at[pl.ds(TAIL - RIM, RIM), :], r.xp.at[pl.ds(0, RIM), :],
-                   r.rim_s.at[0], r.rim_r.at[0], ahead),
-            to_seq(r.rimb.at[pl.ds(TAIL - RIM, RIM), :], r.bp.at[pl.ds(0, RIM), :],
-                   r.rim_s.at[1], r.rim_r.at[1], ahead),
-        )
-
-        @pl.when(at < n_seq - 1)
-        def _():
-            for c in rims:
-                c.start()
+        r.carry[...] = jnp.zeros_like(r.carry)
 
         @pl.when(at == 0)
         def _():
-            r.xp[0:RIM, :] = jnp.zeros((RIM, inner), F32)
-            r.bp[0:RIM, :] = jnp.zeros((RIM, 2 * LANES), F32)
+            r.tail[0:TAIL, own] = jnp.zeros((TAIL, part), BF16)
+
+        @pl.when(at > 0)
+        def _():
+            got(r.tail.at[pl.ds(0, TAIL), own], r.rim_r.at[0])
+
+        got(r.tail.at[pl.ds(0, TAIL), own], r.rim_r.at[1])
+        for lanes, q in ((before, right), (after, left), (far_side, opp)):
+            to_tp(r.tail.at[:, own], r.tail.at[:, lanes], r.tail_s.at[0], r.tail_r.at[0], q).start()
+
+        @pl.when(late == 1)
+        def _():
+            send_own(1)
+
+        def project_rims():
+            got(r.tail.at[:, known], r.tail_r.at[0])
+            spots = ((0, TAIL - RIM), (half_rows + RIM, 2 * TAIL - RIM))
+            for n in range(inner // ntile):
+                lanes = slice(n * ntile, (n + 1) * ntile)
+                ahead_x = dot(r.tail[...], r.wx[:, lanes])
+                for to, row in spots:
+                    r.xp[to : to + RIM, lanes] = ahead_x[row : row + RIM, :]
+            ahead_b = dot(r.tail[...], r.wb[...])
+            for to, row in spots:
+                r.bp[to : to + RIM, :] = ahead_b[row : row + RIM, :]
+
+        def padded(b):
+            return pl.ds(pl.multiple_of(b * piece + RIM + (b // hp) * RIM, RIM), piece)
 
         def times_step(lanes, mine):
             return lax.dot_general(
@@ -301,7 +375,7 @@
 
         def project_known(b):
             mine = prows(b)
-            later = pl.ds(pl.multiple_of(b * piece + RIM, 8), piece)
+            later = padded(b)
             r.bp[later, :] = dot(r.h[mine, known], r.wb[known, :])
             r.sp[mine, :] = times_step(known, mine)
 
@@ -311,7 +385,7 @@
 
         def project_far(b):
             mine = prows(b)
-            later = pl.ds(pl.multiple_of(b * piece + RIM, 8), piece)
+            later = padded(b)
             r.bp[later, :] = r.bp[later, :] + dot(r.h[mine, far_side], r.wb[far_side, :])
             r.sp[mine, :] = r.sp[mine, :] + times_step(far_side, mine)
 
@@ -322,14 +396,15 @@
                 )
 
         def project_gate(b):
-            mine = pl.ds(b * (rows // 2), rows // 2)
+            mine = brows(b)
             for n in range(inner // ntile):
                 lanes = slice(n * ntile, (n + 1) * ntile)
                 r.gs[mine, lanes] = half_silu(dot(r.h[mine, :], r.wg[:, lanes])).astype(BF16)
 
         def conv_and_state(k):
             mine = crows(k)
-            window = pl.ds(pl.multiple_of(k * CHUNK, CHUNK), CHUNK + RIM)
+            seg = k // hc
+            window = pl.ds(pl.multiple_of(k * CHUNK + seg * RIM, RIM), CHUNK + RIM)
             bc = conv_silu(r.bp[window, :], r.bcc_w[...], r.bcc_b[...])
             b_t = bc[:, :LANES].T.astype(BF16)
             c_in = bc[:, LANES:].astype(BF16)
@@ -343,9 +418,9 @@
             end = cum[CHUNK - 1 :, :]
             rest = jnp.exp(end - cum) * step
             r.cum[...] = cum
-            r.cd[mine, :] = cum + r.run[...]
-            r.run[...] = r.run[...] + end
-            r.yi[...] = dot(c_in, r.state[...].astype(BF16))
+            r.cd[mine, :] = cum + r.run[seg]
+            r.run[seg] = r.run[seg] + end
+            r.yi[...] = dot(c_in, r.state[seg].astype(BF16))
             low = lax.broadcasted_iota(jnp.int32, (CHUNK, LANES), 1) < HEAD
             ends = jnp.exp(end)
             for k2 in range(pairs):
@@ -357,7 +432,7 @@
                 r.xc[:, lanes] = x.astype(BF16)
                 r.fed[:CHUNK, lanes] = jnp.where(low, x_step, 0.0).astype(BF16)
                 r.fed[CHUNK:, lanes] = jnp.where(low, 0.0, x_step).astype(BF16)
-            r.state[...] = r.dexp[...] * r.state[...] + dot(b_t, r.xw[...])
+            r.state[seg] = r.dexp[...] * r.state[seg] + dot(b_t, r.xw[...])
 
         def within(k):
             mine = crows(k)
@@ -380,7 +455,6 @@
                     y + jnp.exp(both) * r.yi[:, lanes] + kept * r.xc[:, lanes].astype(F32)
                 )
 
-        n_y, n_x, n_c = split
         y, x, core = at // (n_x * n_c), lax.rem(at // n_c, n_x), lax.rem(at, n_c)
         apart = sorted(
             ((dy, dx, dc) for dy in range(n_y) for dx in range(n_x) for dc in range(n_c)),
@@ -392,85 +466,52 @@
             px = lax.rem(x + d[1], n_x)
             return (py * n_x + px) * n_c + lax.rem(core + d[2], n_c)
 
-        def send_states():
+        others = pl.ds(0, n_seq - 1)
+
+        def send_states(seg):
             for k2 in range(pairs):
                 lanes = slice(k2 * LANES, (k2 + 1) * LANES)
-                r.dexp[:, lanes] = jnp.exp(pair_of(r.run[...], k2, 1)[2])
+                r.dexp[:, lanes] = jnp.exp(pair_of(r.run[seg], k2, 1)[2])
             for j in range(lane_parts):
-                r.dtx[j] = r.dexp[:, j * slice_lanes : (j + 1) * slice_lanes]
+                r.dtx[seg, j] = r.dexp[:, j * slice_lanes : (j + 1) * slice_lanes]
             for j in range(n_seq):
                 top = (j // lane_parts) * slice_rows
                 lane = (j % lane_parts) * slice_lanes
-                r.stx[j] = r.state[top : top + slice_rows, lane : lane + slice_lanes].astype(BF16)
+                r.stx[seg, j] = r.state[
+                    seg, top : top + slice_rows, lane : lane + slice_lanes
+                ].astype(BF16)
             for d in apart:
                 q = seq_of(d)
-                to_seq(r.dtx.at[lax.rem(q, lane_parts)], r.drx.at[at],
-                       r.dc_s.at[0], r.dc_r.at[0], q).start()
-                to_seq(r.stx.at[q], r.srx.at[at], r.st_s.at[0], r.st_r.at[0], q).start()
-
-        def gather_step(b, _):
-            @pl.when(b < pieces)
-            def _():
-                got(r.h.at[prows(b), before], r.own_pr.at[b])
-                rel_p(b).start()
-                got(r.h.at[prows(b), after], r.own_mr.at[b])
-                rel_m(b).start()
-
-                @pl.when(b + 2 < pieces)
-                def _():
-                    own_p(b + 2).start()
-                    own_m(b + 2).start()
-
-                project_known(b)
-
-            @pl.when(b == 1)
-            def _():
-                @pl.when(at > 0)
-                def _():
-                    got(r.xp.at[pl.ds(0, RIM), :], r.rim_r.at[0])
-                    got(r.bp.at[pl.ds(0, RIM), :], r.rim_r.at[1])
-
-            @pl.when(b > 0)
-            def _():
-                done = b - 1
-                got(r.h.at[phalf(done, 0), far_side], r.rel_pr.at[done])
-                got(r.h.at[phalf(done, 1), far_side], r.rel_mr.at[done])
-                project_far(done)
-                conv_and_state(done)
-
-                @pl.when(b == pieces)
-                def _():
-                    send_states()
-
-                within(done)
-
-            return 0
-
-        lax.fori_loop(0, pieces + 1, gather_step, 0)
-        r.srx[at] = r.stx[at]
-        r.drx[at] = r.dtx[lax.rem(at, lane_parts)]
-        others = pl.ds(0, n_seq - 1)
-        got(r.wg, r.load.at[4])
-        project_gate(0)
-        got(r.drx.at[others], r.dc_r.at[0])
-        got(r.srx.at[others], r.st_r.at[0])
-
-        def scan(j, before):
-            r.ptx[j] = before.astype(BF16)
-            return r.drx[j] * before + r.srx[j].astype(F32)
-
-        lax.fori_loop(0, n_seq, scan, jnp.zeros((slice_rows, slice_lanes), F32))
-
-        for d in apart:
-            q = seq_of(d)
-            to_seq(r.ptx.at[q], r.prx.at[at], r.pf_s.at[0], r.pf_r.at[0], q).start()
-        r.prx[at] = r.ptx[at]
-        project_gate(1)
-        got(r.prx.at[others], r.pf_r.at[0])
-        for j in range(n_seq):
-            top = (j // lane_parts) * slice_rows
-            lane = (j % lane_parts) * slice_lanes
-            r.sin[top : top + slice_rows, lane : lane + slice_lanes] = r.prx[j].astype(F32)
+                to_seq(r.dtx.at[seg, lax.rem(q, lane_parts)], r.drx.at[seg, at],
+                       r.dc_s.at[seg], r.dc_r.at[seg], q).start()
+                to_seq(r.stx.at[seg, q], r.srx.at[seg, at],
+                       r.st_s.at[seg], r.st_r.at[seg], q).start()
+            r.srx[seg, at] = r.stx[seg, at]
+            r.drx[seg, at] = r.dtx[seg, lax.rem(at, lane_parts)]
+
+        def send_prefixes(seg):
+            got(r.drx.at[seg, others], r.dc_r.at[seg])
+            got(r.srx.at[seg, others], r.st_r.at[seg])
+
+            def scan(i, passed):
+                base = seg * (n_seq // 2) + i // 2
+                j = base + lax.rem(i, 2) * (mate_of(base) - base)
+                r.ptx[seg, j] = passed.astype(BF16)
+                return r.drx[seg, j] * passed + r.srx[seg, j].astype(F32)
+
+            r.carry[...] = lax.fori_loop(0, n_seq, scan, r.carry[...])
+            for d in apart:
+                q = seq_of(d)
+                to_seq(r.ptx.at[seg, q], r.prx.at[seg, at],
+                       r.pf_s.at[seg], r.pf_r.at[seg], q).start()
+            r.prx[seg, at] = r.ptx[seg, at]
+
+        def take_prefixes(seg):
+            got(r.prx.at[seg, others], r.pf_r.at[seg])
+            for j in range(n_seq):
+                top = (j // lane_parts) * slice_rows
+                lane = (j % lane_parts) * slice_lanes
+                r.sin[top : top + slice_rows, lane : lane + slice_lanes] = r.prx[seg, j].astype(F32)
 
         def stat_to(k, off):
             here = r.stat.at[me, k]
@@ -478,14 +519,14 @@
 
         def gate(k, _):
             mine = crows(k)
-            r.yi[...] = dot(r.cs[mine, :], r.sin[...].astype(BF16))
+            r.yg[...] = dot(r.cs[mine, :], r.sin[...].astype(BF16))
             reach = r.cd[mine, :]
             squares = jnp.zeros((CHUNK, LANES), F32)
             tops = jnp.zeros((CHUNK, LANES), F32)
             for k2 in range(pairs):
                 lanes = slice(k2 * LANES, (k2 + 1) * LANES)
                 _, _, both = pair_of(reach, k2, CHUNK)
-                out = r.ys[mine, lanes] + jnp.exp(both) * r.yi[:, lanes]
+                out = r.ys[mine, lanes] + jnp.exp(both) * r.yg[:, lanes]
                 gated = out * r.gs[mine, lanes].astype(F32)
                 squares = squares + gated * gated
                 gained = gated * r.gain[k2 : k2 + 1, :]
@@ -496,6 +537,63 @@
             for off in range(1, n_tp):
                 stat_to(k, off).start()
             return 0
+
+        lag = hc
+
+        def gather_step(i, _):
+            @pl.when(i == hp + 2)
+            def _():
+                got(r.wg, r.load.at[4])
+                lax.fori_loop(0, half_blocks, lambda b, _: (project_gate(b), 0)[1], 0)
+
+            @pl.when(i < pieces)
+            def _():
+                b = place(i)
+                got(r.h.at[prows(b), before], r.own_pr.at[b])
+                rel_p(b).start()
+                got(r.h.at[prows(b), after], r.own_mr.at[b])
+                rel_m(b).start()
+
+                @pl.when(i + 2 < pieces)
+                def _():
+                    send_own(i + 2)
+
+            @pl.when(i == scan_at)
+            def _():
+                send_prefixes(0)
+
+            @pl.when(i < pieces)
+            def _():
+                @pl.when(i == 0)
+                def _():
+                    got(r.wx, r.load.at[2])
+                    got(r.wb, r.load.at[3])
+
+                project_known(place(i))
+
+            @pl.when(i == 1)
+            def _():
+                project_rims()
+
+            @pl.when(i > 0)
+            def _():
+                done = place(i - 1)
+                got(r.h.at[phalf(done, 0), far_side], r.rel_pr.at[done])
+                got(r.h.at[phalf(done, 1), far_side], r.rel_mr.at[done])
+                project_far(done)
+                conv_and_state(done)
+
+                @pl.when(lax.rem(done + 1, hp) == 0)
+                def _():
+                    send_states(done // hp)
+
+                @pl.when(i < pieces)
+                def _():
+                    within(done)
+
+            return 0
+
+        lax.fori_loop(0, pieces + 1, gather_step, 0)
 
         most = r.hist[0]
         for i in range(1, r.hist.shape[0]):
@@ -534,33 +632,72 @@
             return to_tp(r.tr.at[khalf(k, 1), :], r.rr.at[kept_half(k), :],
                          r.far_ms.at[0], r.far_mr.at[k], left)
 
-        def near_p(b):
-            return to_tp(r.txp.at[brows(b), :], r.rxp.at[brows(b), :],
-                         r.near_ps.at[0], r.near_pr.at[b], right)
-
-        def near_m(b):
-            return to_tp(r.txm.at[brows(b), :], r.rxm.at[brows(b), :],
-                         r.near_ms.at[0], r.near_mr.at[b], left)
-
-        lag = min(4, chunks)
-
-        def far(k, _):
-            @pl.when(k < chunks)
-            def _():
-                gate(k, 0)
+        def near_p(k):
+            return to_tp(r.txp.at[crows(k), :], r.rxp.at[crows(k), :],
+                         r.near_ps.at[0], r.near_pr.at[k], right)
+
+        def near_m(k):
+            return to_tp(r.txm.at[crows(k), :], r.rxm.at[crows(k), :],
+                         r.near_ms.at[0], r.near_mr.at[k], left)
+
+        def far(k, seg):
+            @pl.when((seg == 1) & (k == hc // 2))
+            def _():
+                lax.fori_loop(held, first_near, near, 0)
 
             @pl.when(k >= lag)
             def _():
-                ready = k - lag
+                ready = seg * hc + k - lag
                 norm(ready)
                 mine = crows(ready)
                 r.tr[mine, :] = dot(r.gs[mine, :], r.wo[:, cols(opp)]).astype(BF16)
                 far_p(ready).start()
                 far_m(ready).start()
 
+            @pl.when(k < hc)
+            def _():
+                gate(seg * hc + k, 0)
+
+            return seg
+
+        def order_of(i):
+            past = (i + chunks - first_near) // chunks
+            end = (i + 1) // chunks
+            return i + (1 - late) * (past - end * (chunks - first_near))
+
+        def near(i, _):
+            k = order_of(i)
+            mine = crows(k)
+            r.txp[mine, :] = dot(r.gs[mine, :], r.wo[:, cols(right)]).astype(BF16)
+            r.txm[mine, :] = dot(r.gs[mine, :], r.wo[:, cols(left)]).astype(BF16)
+            top = khalf(k, 0)
+            got(r.rl.at[kept_half(k), :], r.far_pr.at[k])
+            r.txp[top, :] = (
+                r.txp[top, :].astype(F32) + r.rl[kept_half(k), :].astype(F32)
+            ).astype(BF16)
+            near_p(k).start()
+            low = khalf(k, 1)
+            got(r.rr.at[kept_half(k), :], r.far_mr.at[k])
+            r.txm[low, :] = (
+                r.txm[low, :].astype(F32) + r.rr[kept_half(k), :].astype(F32)
+            ).astype(BF16)
+            near_m(k).start()
             return 0
 
-        lax.fori_loop(0, chunks + lag, far, 0)
+        def segment(seg, _):
+            take_prefixes(seg)
+            lax.fori_loop(0, hc + lag, far, seg)
+
+            @pl.when(seg == 0)
+            def _():
+                send_prefixes(1)
+                within(chunks - 1)
+                lax.fori_loop(half_blocks, blocks, lambda b, _: (project_gate(b), 0)[1], 0)
+                lax.fori_loop(0, held, near, 0)
+
+            return 0
+
+        lax.fori_loop(0, 2, segment, 0)
         r.pkt[...] = r.peak[...]
 
         def peak_to(off):
@@ -574,41 +711,40 @@
         lax.fori_loop(1, n_seq, peak_send, 0)
         r.pkr[at] = r.peak[...]
 
-        def near(b, _):
-            mine = brows(b)
-            r.txp[mine, :] = dot(r.gs[mine, :], r.wo[:, cols(right)]).astype(BF16)
-            r.txm[mine, :] = dot(r.gs[mine, :], r.wo[:, cols(left)]).astype(BF16)
-            for j in range(per):
-                k = b * per + j
-                top = khalf(k, 0)
-                got(r.rl.at[kept_half(k), :], r.far_pr.at[k])
-                r.txp[top, :] = (
-                    r.txp[top, :].astype(F32) + r.rl[kept_half(k), :].astype(F32)
-                ).astype(BF16)
-            near_p(b).start()
-            for j in range(per):
-                k = b * per + j
-                low = khalf(k, 1)
-                got(r.rr.at[kept_half(k), :], r.far_mr.at[k])
-                r.txm[low, :] = (
-                    r.txm[low, :].astype(F32) + r.rr[kept_half(k), :].astype(F32)
-                ).astype(BF16)
-            near_m(b).start()
+        lax.fori_loop(first_near, chunks, near, 0)
+
+        def back(j):
+            here = pl.ds(pl.multiple_of(j * CHUNK, CHUNK), CHUNK)
+            return to_seq(r.otx.at[here, :], r.orx.at[here, :],
+                          r.out_s.at[0], r.out_r.at[j], mate)
+
+        def finish(i, _):
+            k = order_of(i)
+            mine = crows(k)
+            total = dot(r.gs[mine, :], r.wo[:, cols(me)])
+            got(r.rxp.at[mine, :], r.near_pr.at[k])
+            got(r.rxm.at[mine, :], r.near_mr.at[k])
+            total = total + (r.rxp[mine, :].astype(F32) + r.rxm[mine, :].astype(F32))
+            out = (total * unscale[0:1, 0:1]).astype(BF16)
+            j = lax.rem(k, hc)
+            here = pl.ds(pl.multiple_of(j * CHUNK, CHUNK), CHUNK)
+
+            @pl.when(k // hc == late)
+            def _():
+                r.mixed[here, :] = out
+
+            @pl.when(k // hc != late)
+            def _():
+                r.otx[here, :] = out
+                back(j).start()
+
             return 0
 
-        lax.fori_loop(0, blocks, near, 0)
-
-        def finish(b, _):
-            mine = brows(b)
-            total = dot(r.gs[mine, :], r.wo[:, cols(me)])
-            got(r.rxp.at[mine, :], r.near_pr.at[b])
-            got(r.rxm.at[mine, :], r.near_mr.at[b])
-            total = total + (r.rxp[mine, :].astype(F32) + r.rxm[mine, :].astype(F32))
-            r.mixed[mine, :] = (total * unscale[0:1, 0:1]).astype(BF16)
-            return 0
-
-        lax.fori_loop(0, blocks, finish, 0)
-
+        lax.fori_loop(0, chunks, finish, 0)
+        for j in range(hc):
+            got(r.orx.at[pl.ds(j * CHUNK, CHUNK), :], r.out_r.at[j])
+            to = half_rows + j * CHUNK
+            r.mixed[to : to + CHUNK, :] = r.orx[j * CHUNK : (j + 1) * CHUNK, :]
         got(r.pkr.at[others], r.pk_r.at[0])
         top = lax.fori_loop(0, n_seq, lambda j, v: jnp.maximum(v, r.pkr[j]), r.peak[...])
         lane = lax.broadcasted_iota(jnp.int32, r.news.shape, 1)
@@ -621,19 +757,22 @@
 
         @pl.when(at < n_seq - 1)
         def _():
-            for c in rims:
-                c.wait_send()
-
+            rims[0].wait_send()
+
+        rims[1].wait_send()
         half_own = r.h.at[pl.ds(0, rows // 2), own]
         for view, sem in (
             (r.h.at[:, own], r.own_ps), (r.h.at[:, own], r.own_ms),
             (half_own, r.rel_ps), (half_own, r.rel_ms),
             (r.rl, r.far_ps), (r.rr, r.far_ms), (r.txp, r.near_ps), (r.txm, r.near_ms),
-            (r.drx.at[others], r.dc_s), (r.srx.at[others], r.st_s),
-            (r.prx.at[others], r.pf_s), (r.pkr.at[others], r.pk_s),
+            (r.swap, r.swap_s), (r.otx, r.out_s), (r.pkr.at[others], r.pk_s),
             (r.stat.at[pl.ds(0, n_tp - 1)], r.sa_s),
         ):
             got(view, sem.at[0])
+        for seg in range(2):
+            got(r.drx.at[seg, others], r.dc_s.at[seg])
+            got(r.srx.at[seg, others], r.st_s.at[seg])
+            got(r.prx.at[seg, others], r.pf_s.at[seg])
 
     hbm = pl.BlockSpec(memory_space=pl.ANY)
     local = pl.BlockSpec(memory_space=pltpu.VMEM)
@@ -645,9 +784,9 @@
             pltpu.VMEM((rows, part), BF16),
             pltpu.VMEM((1, 16), F32),
         ),
-        in_specs=[hbm] * 4 + [local] * 9 + [hbm, scalars],
+        in_specs=[hbm] * 14 + [scalars],
         out_specs=(local, local),
-        scratch_shapes=[pltpu.VMEM(*v) for v in vmem.values()]
+        scratch_shapes=[pltpu.VMEM(*v) for v in (*vmem.values(), *small.values())]
         + [pltpu.SemaphoreType.DMA((n,)) for n in dma.values()],
         compiler_params=pltpu.CompilerParams(
             collective_id=0, has_side_effects=True, vmem_limit_bytes=65_650_000

time: 124 us -> 118 us (0.952)
  Pallas kernels: 122 us -> 115 us
    pallas_call x1, Pallas kernels: 122 us -> 115 us  [shards(): call(hidden, gate_proj, input_proj, bc_proj, step_proj.T, step_bias[None]...]
where the time goes in v3:
time: 118 us; the launch traced here: 117 us
  Pallas kernels  115 us (97%)
  local copies, waits for them, and re-layouts  1.57 us (1%)
    pallas_call x1, Pallas kernels, shards(): call(hidden, gate_proj, input_proj, bc_proj, step_proj.T, step_bias[None]...  115 us

profile of v3, /device:TPU:0, one launch (start us, length us, event | category | flops | bytes accessed | tf_op | source)
XLA Modules:
  0.0 116.9 jit_solution(11931195096117451469)
XLA Ops:
  0.6 114.7 %layer.1 = (bf16[1024,640]{1,0:T(8,128)(2,1)S(1)}, f32[1,16]{1,0:T(1,128)S(1)}) custom-call(bf16[1024,640]{1,0:T(8,128)(2,1)} %refs_0_.1, bf16[2560,1280]{1,0:T(8,128)(2,1)} %refs_1_.1, bf16[2560,1280]{1,0:T(8,128)(2,1)} %refs_2_.1, bf16[2560,256]{1,0:T(8,128)(2,1)} %refs_3_.1, bf16[20,2560]{1,0:T(8,128)(2,1)} %bitcast.9, f32[1,20]{1,0:T(1,128)} %bitcast.13, ...), custom_call_target="tpu_custom_call" | custom-call | tf_op jit(solution)/shard_map/layer/pallas_call | solution.py:808
  115.3 1.1 copy.19
  116.4 0.5 copy.20

commit v4 on v3

--- a/solution.py
+++ b/solution.py
@@ -216,6 +216,13 @@
         for c in first:
             c.start()
 
+        smalls = [
+            pltpu.make_async_copy(getattr(r, k + "_in"), getattr(r, k), r.smalls.at[i])
+            for i, k in enumerate(small)
+        ]
+        for c in smalls:
+            c.start()
+
         def by_rows(src, dst, i):
             return [
                 load(src.at[pl.ds(pl.multiple_of(q * part, LANES), part), :],
@@ -227,11 +234,6 @@
             by_rows(r.in_w, r.wx, 2) + by_rows(r.bc_w, r.wb, 3) + by_rows(r.gate_w, r.wg, 4)
             + [load(r.out_w, r.wo, 5)]
         )
-
-        smalls = [
-            pltpu.make_async_copy(getattr(r, k + "_in"), getattr(r, k), r.smalls.at[i])
-            for i, k in enumerate(small)
-        ]
 
         barrier = pltpu.get_barrier_semaphore()
         for off in range(1, n_tp):
@@ -320,7 +322,7 @@
 
         for j in range(hp):
             swap(j).start()
-        for c in (*smalls, *weights):
+        for c in weights:
             c.start()
         for c in smalls:
             c.wait()
@@ -587,9 +589,7 @@
                 def _():
                     send_states(done // hp)
 
-                @pl.when(i < pieces)
-                def _():
-                    within(done)
+                within(done)
 
             return 0
 
@@ -691,7 +691,6 @@
             @pl.when(seg == 0)
             def _():
                 send_prefixes(1)
-                within(chunks - 1)
                 lax.fori_loop(half_blocks, blocks, lambda b, _: (project_gate(b), 0)[1], 0)
                 lax.fori_loop(0, held, near, 0)
 

time: 118 us -> 118 us (level)
  no operation moved by 1% of the time
where the time goes in v4:
time: 118 us; the launch traced here: 117 us
  Pallas kernels  115 us (97%)
  local copies, waits for them, and re-layouts  1.57 us (1%)
    pallas_call x1, Pallas kernels, shards(): call(hidden, gate_proj, input_proj, bc_proj, step_proj.T, step_bias[None]...  115 us

profile of v4, /device:TPU:0, one launch (start us, length us, event | category | flops | bytes accessed | tf_op | source)
XLA Modules:
  0.0 116.9 jit_solution(14046444497221372741)
XLA Ops:
  0.6 114.7 %layer.1 = (bf16[1024,640]{1,0:T(8,128)(2,1)S(1)}, f32[1,16]{1,0:T(1,128)S(1)}) custom-call(bf16[1024,640]{1,0:T(8,128)(2,1)} %refs_0_.1, bf16[2560,1280]{1,0:T(8,128)(2,1)} %refs_1_.1, bf16[2560,1280]{1,0:T(8,128)(2,1)} %refs_2_.1, bf16[2560,256]{1,0:T(8,128)(2,1)} %refs_3_.1, bf16[20,2560]{1,0:T(8,128)(2,1)} %bitcast.9, f32[1,20]{1,0:T(1,128)} %bitcast.13, ...), custom_call_target="tpu_custom_call" | custom-call | tf_op jit(solution)/shard_map/layer/pallas_call | solution.py:807
  115.3 1.1 copy.19
  116.4 0.5 copy.20
